TPU v7x, 32 devices: a 4x4x1 block of a 4x4x8 slice. The times are simulated.
32 devices in a mesh: rep: 2 (over z, core), dp: 16 (over x, y).
Axes of the slice: x: 4, y: 4, z: 1, core: 2. Of those that a mesh axis runs over, the one named last changes fastest.
The devices are a block of a 4x4x8 slice.
Arguments:
- x: bfloat16 [32, 2048, 1024], P(('rep', 'dp')), parts along dimension 0
- dy: bfloat16 [32, 2048, 1024], P(('rep', 'dp')), parts along dimension 0
- w_gate: bfloat16 [2, 1024, 3200], replicated
- w_up: bfloat16 [2, 1024, 3200], replicated
- w_down: bfloat16 [2, 3200, 1024], replicated
- m_w_gate: float32 [2, 1024, 3200], P(None, 'dp')
- m_w_up: float32 [2, 1024, 3200], P(None, 'dp')
- m_w_down: float32 [2, 3200, 1024], P(None, 'dp')
- v_w_gate: float32 [2, 1024, 3200], P(None, 'dp')
- v_w_up: float32 [2, 1024, 3200], P(None, 'dp')
- v_w_down: float32 [2, 3200, 1024], P(None, 'dp')
Outputs:
- output 1: bfloat16 [4, 1024, 3200], P('rep'), parts along dimension 0
- output 2: bfloat16 [4, 1024, 3200], P('rep'), parts along dimension 0
- output 3: bfloat16 [4, 3200, 1024], P('rep'), parts along dimension 0
- output 4: float32 [4, 1024, 3200], P('rep', 'dp'), parts along dimension 0
- output 5: float32 [4, 1024, 3200], P('rep', 'dp'), parts along dimension 0
- output 6: float32 [4, 3200, 1024], P('rep', 'dp'), parts along dimension 0
- output 7: float32 [4, 1024, 3200], P('rep', 'dp'), parts along dimension 0
- output 8: float32 [4, 1024, 3200], P('rep', 'dp'), parts along dimension 0
- output 9: float32 [4, 3200, 1024], P('rep', 'dp'), parts along dimension 0
There are 2 independent parts. A program takes and returns all parts, laid end to end along the dimension named above; an argument that names none is the same for every part.
All inputs are finite; a program needn't handle non-finite values.
Results may differ from a plain program's by a relative error of at most 0.022.
Values are sent between devices in bfloat16 or wider.
A program may use at most 768 MiB of HBM per device.

v0:
```python
import jax
import jax.numpy as jnp
from jax import lax

NAMES = ("w_gate", "w_up", "w_down")


def matmul(a, w):
    return jnp.dot(a, w, preferred_element_type=jnp.float32).astype(jnp.bfloat16)


def normed(h):
    wide = h.astype(jnp.float32)
    scale = lax.rsqrt(jnp.mean(wide**2, -1, keepdims=True) + 1e-6)
    return (wide * scale).astype(jnp.bfloat16)


def layer(h, w):
    a = normed(h)
    gate = jnp.dot(a, w["w_gate"], preferred_element_type=jnp.float32)
    up = jnp.dot(a, w["w_up"], preferred_element_type=jnp.float32)
    return h + matmul((jax.nn.silu(gate) * up).astype(jnp.bfloat16), w["w_down"])


def adamw(w, m, v, g):
    m = 0.9 * m + 0.1 * g
    v = 0.95 * v + 0.05 * g * g
    step = m * lax.rsqrt(v + 1e-8) + 0.1 * w
    return (w - 0.02 * step).astype(jnp.bfloat16), m, v


def clipped(gradients, sum_of_squares, count):
    factor = jnp.minimum(1.0, 0.5 * lax.rsqrt(sum_of_squares / count + 1e-30))
    return [g * factor for g in gradients]


def stack(weights, h):
    for number in range(weights["w_gate"].shape[0]):
        h = layer(h, {name: w[number] for name, w in weights.items()})
    return h


def solution(mesh):
    groups = mesh.shape["rep"]

    def step(x, dy, *arrays):
        weights, m, v = (arrays[i : i + 3] for i in (0, 3, 6))
        x, dy = (t.reshape(groups, -1, *t.shape[1:]) for t in (x, dy))

        def of_a_group(x, dy):
            _, back = jax.vjp(lambda w: stack(w, x), dict(zip(NAMES, weights, strict=True)))
            by_weights = back(dy)[0]
            gradients = [by_weights[name].astype(jnp.float32) for name in NAMES]
            gradients = clipped(gradients, sum(jnp.sum(g * g) for g in gradients), sum(g.size for g in gradients))
            new = [adamw(w.astype(jnp.float32), m, v, g) for w, m, v, g in zip(weights, m, v, gradients, strict=True)]
            return tuple(one[which] for which in range(3) for one in new)

        return tuple(t.reshape(-1, *t.shape[2:]) for t in jax.vmap(of_a_group)(x, dy))

    return step
```

profile of v0, /device:TPU:97, one launch (start us, length us, event | category | flops | bytes accessed | tf_op | source)
XLA Modules:
  0.0 1112.5 jit_solution(7052366283738770545)
XLA Ops:
  7.2 0.1 reduce-scatter.31.cloned.1.call-start
  7.3 3.1 fusion.47
  10.3 6.6 copy
  17.0 22.0 %fusion.67 = f32[2048,3200]{1,0:T(8,128)} fusion(bf16[2,1024,3200]{2,1,0:T(8,128)(2,1)} %param, bf16[1,2048,1024]{2,1,0:T(8,128)(2,1)} %param.2, f32[2048]{0:T(1024)S(1)} %add_rsqrt_fusion), kind=kOutput, calls=%fused_computation.79 | convolution fusion | flops 13428064256 | bytes 36970496 | tf_op jit(solution)/vmap(jvp())/dot_general | solution.py:20
  39.0 18.0 %fusion.65 = f32[2048,3200]{1,0:T(8,128)} fusion(bf16[2,1024,3200]{2,1,0:T(8,128)(2,1)S(1)} %bitcast.344, bf16[1,2048,1024]{2,1,0:T(8,128)(2,1)S(1)} %copy-done.1, f32[2048]{0:T(1024)S(1)} %add_rsqrt_fusion), kind=kOutput, calls=%fused_computation.77 | convolution fusion | flops 13428064256 | bytes 36970496 | tf_op jit(solution)/vmap(jvp())/dot_general | solution.py:21
  57.0 22.9 %fusion.26 = bf16[2048,3200]{1,0:T(8,128)(2,1)} fusion(f32[2048,3200]{1,0:T(8,128)} %fusion.65, f32[2048,3200]{1,0:T(8,128)} %fusion.67), kind=kLoop, calls=%fused_computation.41 | loop fusion | flops 39321600 | bytes 65536000
  79.9 22.1 %fusion.51 = (f32[2048]{0:T(1024)S(1)}, bf16[1,1,2048,1024]{2,3,1,0:T(8,128)(2,1)}) fusion(bf16[2048,3200]{1,0:T(8,128)(2,1)} %fusion.26, bf16[2,3200,1024]{2,1,0:T(8,128)(2,1)} %param.4, bf16[1,2048,1024]{1,2,0:T(8,128)(2,1)} %copy), kind=kOutput, calls=%fused_computation.62 | convolution fusion | flops 13432256512 | bytes 28057600 | tf_op jit(solution)/vmap(jvp())/dot_general | solution.py:9
  102.1 0.6 copy-done.6
  102.6 23.4 %fusion.54 = f32[2048,3200]{1,0:T(8,128)} fusion(bf16[2,1024,3200]{2,1,0:T(8,128)(2,1)} %param, bf16[1,1,2048,1024]{2,3,1,0:T(8,128)(2,1)} %get-tuple-element.10, f32[2048]{0:T(1024)S(1)} %bitcast.346), kind=kOutput, calls=%fused_computation.66 | convolution fusion | flops 13428064256 | bytes 36970496 | tf_op jit(solution)/vmap(jvp())/dot_general | solution.py:20
  126.1 20.8 %fusion.58 = f32[2048,3200]{1,0:T(8,128)} fusion(bf16[2,1024,3200]{2,1,0:T(8,128)(2,1)} %param.3, bf16[1,1,2048,1024]{2,3,1,0:T(8,128)(2,1)S(1)} %copy-done.3, f32[2048]{0:T(1024)S(1)} %bitcast.347), kind=kOutput, calls=%fused_computation.70 | convolution fusion | flops 13428064256 | bytes 36970496 | tf_op jit(solution)/vmap(jvp())/dot_general | solution.py:21
  146.8 28.6 %fusion.35 = f32[1,3200,1024]{2,1,0:T(8,128)} fusion(f32[2048,3200]{1,0:T(8,128)} %fusion.58, f32[2048,3200]{1,0:T(8,128)} %fusion.54, bf16[1,2048,1024]{2,1,0:T(8,128)(2,1)} %param.5), kind=kOutput, calls=%fused_computation.52 | convolution fusion | flops 13461094400 | bytes 69730304 | tf_op jit(solution)/vmap(transpose(jvp()))/dot_general | solution.py:9
  175.4 0.1 reduce-scatter.31.cloned.1.call-update
  175.4 0.1 reduce-scatter.33.cloned.1.call-start
  175.5 6.6 copy.1
  182.1 20.8 %convolution_convert_fusion.1 = bf16[2048,3200]{1,0:T(8,128)(2,1)} fusion(bf16[2,3200,1024]{2,1,0:T(8,128)(2,1)} %param.4, bf16[1,2048,1024]{2,1,0:T(8,128)(2,1)} %param.5), kind=kOutput, calls=%fused_computation.36 | convolution fusion | flops 13428326400 | bytes 23855104 | tf_op jit(solution)/vmap(transpose(jvp()))/dot_general | solution.py:9
  202.9 26.9 %fusion.6 = bf16[2048,3200]{1,0:T(8,128)(2,1)} fusion(f32[2048,3200]{1,0:T(8,128)} %fusion.54, f32[2048,3200]{1,0:T(8,128)} %fusion.58, bf16[2048,3200]{1,0:T(8,128)(2,1)} %convolution_convert_fusion.1), kind=kLoop, calls=%fused_computation.11 | loop fusion | flops 78643200 | bytes 78643200
  229.7 22.5 %fusion.24 = bf16[2048,1024]{0,1:T(8,128)(2,1)} fusion(bf16[2048,3200]{1,0:T(8,128)(2,1)} %convolution_convert_fusion.1, f32[2048,3200]{1,0:T(8,128)} %fusion.54, bf16[2,1024,3200]{2,1,0:T(8,128)(2,1)} %param.3), kind=kOutput, calls=%fused_computation.34 | convolution fusion | flops 13461094400 | bytes 50069504 | tf_op jit(solution)/vmap(transpose(jvp()))/dot_general | solution.py:21
  252.2 23.3 %fusion.53 = (f32[2048]{0:T(1024)S(1)}, bf16[2048,1024]{0,1:T(8,128)(2,1)}) fusion(bf16[1,1,2048,1024]{2,3,1,0:T(8,128)(2,1)} %get-tuple-element.10, bf16[2048,1024]{0,1:T(8,128)(2,1)} %fusion.24, bf16[2048,3200]{1,0:T(8,128)(2,1)} %fusion.6, bf16[2,1024,3200]{2,1,0:T(8,128)(2,1)} %param), kind=kOutput, calls=%fused_computation.64 | convolution fusion | flops 13432256512 | bytes 32251904 | tf_op jit(solution)/vmap(transpose(jvp()))/dot_general | solution.py:20
  275.6 5.3 fusion.81
  280.9 2.0 copy-done.4
  282.9 19.7 %convolution_bitcast_fusion.1 = f32[1,3200,1024]{2,1,0:T(8,128)} fusion(bf16[2048,3200]{1,0:T(8,128)(2,1)} %fusion.26, bf16[2048,1024]{0,1:T(8,128)(2,1)S(1)} %fusion.81), kind=kOutput, calls=%fused_computation.57 | convolution fusion | flops 13421772800 | bytes 30408704 | tf_op jit(solution)/vmap(transpose(jvp()))/dot_general | solution.py:9
  302.6 0.1 reduce-scatter.33.cloned.1.call-update
  302.7 0.1 reduce-scatter.27.cloned.1.call-start
  302.7 26.0 %fusion.38 = f32[1,1024,3200]{2,1,0:T(8,128)} fusion(bf16[2048,3200]{1,0:T(8,128)(2,1)} %convolution_convert_fusion.1, f32[2048,3200]{1,0:T(8,128)} %fusion.54, bf16[1,1,2048,1024]{2,3,1,0:T(8,128)(2,1)} %get-tuple-element.10, f32[2048]{0:T(1024)S(1)} %bitcast.349), kind=kOutput, calls=%fused_computation.53 | convolution fusion | flops 13467385856 | bytes 56631296 | tf_op jit(solution)/vmap(transpose(jvp()))/dot_general | solution.py:21
  328.7 0.1 reduce-scatter.27.cloned.1.call-update
  328.8 0.1 reduce-scatter.29.cloned.1.call-start
  328.9 21.0 %convolution_convert_fusion = bf16[2048,3200]{1,0:T(8,128)(2,1)} fusion(bf16[2048,1024]{0,1:T(8,128)(2,1)} %copy-done.4, bf16[2,3200,1024]{2,1,0:T(8,128)(2,1)} %param.4), kind=kOutput, calls=%fused_computation.35 | convolution fusion | flops 13428326400 | bytes 23855104 | tf_op jit(solution)/vmap(transpose(jvp()))/dot_general | solution.py:9
  349.9 24.9 %fusion.41 = f32[1,1024,3200]{2,1,0:T(8,128)} fusion(bf16[2048,3200]{1,0:T(8,128)(2,1)} %convolution_convert_fusion, f32[2048,3200]{1,0:T(8,128)} %fusion.67, bf16[1,2048,1024]{1,2,0:T(8,128)(2,1)S(1)} %copy-done.5, f32[2048]{0:T(1024)S(1)} %copy-done.11), kind=kOutput, calls=%fused_computation.54 | convolution fusion | flops 13467385856 | bytes 56631296 | tf_op jit(solution)/vmap(transpose(jvp()))/dot_general | solution.py:21
  374.7 0.1 reduce-scatter.29.cloned.1.call-update
  374.8 0.1 reduce-scatter.23.cloned.1.call-start
  374.9 22.1 %convolution_bitcast_fusion = f32[1,1024,3200]{2,1,0:T(8,128)} fusion(bf16[2048,3200]{1,0:T(8,128)(2,1)} %fusion.6, bf16[1,1,2048,1024]{2,3,1,0:T(8,128)(2,1)} %get-tuple-element.10, f32[2048]{0:T(1024)S(1)} %bitcast.350), kind=kOutput, calls=%fused_computation.55 | convolution fusion | flops 13428064256 | bytes 30416896 | tf_op jit(solution)/vmap(transpose(jvp()))/dot_general | solution.py:20
  397.0 0.1 reduce-scatter.25.cloned.1.call-start
  397.1 34.8 %fusion.44 = f32[1,1024,3200]{2,1,0:T(8,128)} fusion(f32[2048,3200]{1,0:T(8,128)} %fusion.67, f32[2048,3200]{1,0:T(8,128)} %fusion.65, bf16[2048,3200]{1,0:T(8,128)(2,1)} %convolution_convert_fusion, bf16[1,2048,1024]{1,2,0:T(8,128)(2,1)} %copy, f32[2048]{0:T(1024)S(1)} %copy-done.11), kind=kOutput, calls=%fused_computation.56 | convolution fusion | flops 13500153856 | bytes 82845696 | tf_op jit(solution)/vmap(transpose(jvp()))/dot_general | solution.py:20
  432.0 0.1 all-gather.14.cloned.1.call-start
  432.1 0.5 copy-done.12
  432.6 0.6 dynamic-slice
  433.8 1.2 convert_bitcast_fusion.4
  435.1 1.2 convert_bitcast_fusion.3
  436.3 1.0 fusion.110
  437.3 51.4 %reduce-scatter.27.cloned.1.call-done = f32[1,64,3200]{2,1,0:T(8,128)} async-done(((f32[1,1024,3200]{2,1,0:T(8,128)}), f32[1,64,3200]{2,1,0:T(8,128)}) %reduce-scatter.27.cloned.1.call-update) | async-done | bytes 819216
  488.7 1.2 convert_bitcast_fusion.6
  489.9 91.3 %reduce-scatter.29.cloned.1.call-done = f32[1,64,3200]{2,1,0:T(8,128)} async-done(((f32[1,1024,3200]{2,1,0:T(8,128)}), f32[1,64,3200]{2,1,0:T(8,128)}) %reduce-scatter.29.cloned.1.call-update) | async-done | bytes 819216
  581.1 1.2 convert_bitcast_fusion.5
  582.3 1.0 fusion.109
  583.4 90.3 %reduce-scatter.23.cloned.1.call-done = f32[1,64,3200]{2,1,0:T(8,128)} async-done(((f32[1,1024,3200]{2,1,0:T(8,128)}), f32[1,64,3200]{2,1,0:T(8,128)}) %reduce-scatter.23.cloned.1.call-update) | async-done | bytes 819216
  673.7 1.2 convert_bitcast_fusion.8
  674.9 91.9 %reduce-scatter.25.cloned.1.call-done = f32[1,64,3200]{2,1,0:T(8,128)} async-done(((f32[1,1024,3200]{2,1,0:T(8,128)}), f32[1,64,3200]{2,1,0:T(8,128)}) %reduce-scatter.25.cloned.1.call-update) | async-done | bytes 819216
  766.8 1.2 convert_bitcast_fusion.7
  768.0 1.0 fusion.108
  770.9 32.4 %all-reduce.16 = f32[1]{0:T(128)} all-reduce(f32[1]{0:T(128)} %bitcast.50), channel_id=5, replica_groups=mesh['rep'=2,'dp'=16] {'dp'}, use_global_device_ids=true, to_apply=%region_3.4.clone | all-reduce | flops 1 | bytes 8 | tf_op jit(solution)/vmap()/reduce_sum | solution.py:54
  804.0 5.1 fusion.127
  809.1 0.1 all-gather.10.cloned.1.call-start
  809.2 5.1 fusion.129
  814.3 0.1 all-gather.12.cloned.1.call-start
  814.4 5.1 fusion.128
  819.5 0.1 all-gather.12.cloned.1.call-update
  819.6 80.6 %all-gather.14.cloned.1.call-done = bf16[1,2,3200,1024]{3,2,1,0:T(8,128)(2,1)} async-done(((bf16[1,2,200,1024]{3,2,1,0:T(8,128)(2,1)}), bf16[1,2,3200,1024]{3,2,1,0:T(8,128)(2,1)}) %all-gather.14.cloned.1.call-update) | async-done | bytes 13107216 | tf_op jit(solution)/reshape | solution.py:58
  900.2 89.3 %all-gather.10.cloned.1.call-done = bf16[1,2,1024,3200]{3,2,1,0:T(8,128)(2,1)} async-done(((bf16[1,2,64,3200]{3,2,1,0:T(8,128)(2,1)}), bf16[1,2,1024,3200]{3,2,1,0:T(8,128)(2,1)}) %all-gather.10.cloned.1.call-update) | async-done | bytes 13107216 | tf_op jit(solution)/reshape | solution.py:58
  989.4 89.3 %all-gather.12.cloned.1.call-done = bf16[1,2,1024,3200]{3,2,1,0:T(8,128)(2,1)} async-done(((bf16[1,2,64,3200]{3,2,1,0:T(8,128)(2,1)}), bf16[1,2,1024,3200]{3,2,1,0:T(8,128)(2,1)}) %all-gather.12.cloned.1.call-update) | async-done | bytes 13107216 | tf_op jit(solution)/reshape | solution.py:58
  1078.7 12.7 %copy.9 = bf16[2,1024,3200]{2,1,0:T(8,128)(2,1)} copy(bf16[2,1024,3200]{2,1,0:T(8,128)(2,1)} %bitcast.339) | data formatting | bytes 26214400
  1091.4 6.6 copy.10
  1098.1 1.2 slice-done.1
  1099.2 1.3 slice-done.2
  1100.5 4.9 copy.11
  (49 shorter events, 0.4 us)
Async XLA Ops:
  7.2 426.6 %reduce-scatter.31.cloned.1.call-start = ((), (), s32[]{:S(2)}) async-start(), calls=%async_computation.13 | async-start | bytes 13926400
  10.3 28.7 %slice-start.4 = ((s8[13107200]{0:T(1024)(128)(4,1)}), s8[524288]{0:T(1024)(128)(4,1)S(1)}, s32[]{:S(2)}) async-start(s8[13107200]{0:T(1024)(128)(4,1)} %bitcast.343), calls=%async_computation.19 | async-start | bytes 1048576
  16.9 22.1 %copy-start.10 = (f32[2048]{0:T(1024)}, f32[2048]{0:T(1024)S(1)}, u32[]{:S(2)}) copy-start(f32[2048]{0:T(1024)S(1)} %add_rsqrt_fusion) | copy-start | bytes 24580
  16.9 22.1 %copy-start.1 = (bf16[1,2048,1024]{2,1,0:T(8,128)(2,1)S(1)}, bf16[1,2048,1024]{2,1,0:T(8,128)(2,1)}, u32[]{:S(2)}) copy-start(bf16[1,2048,1024]{2,1,0:T(8,128)(2,1)} %param.2) | copy-start | bytes 12582916
  16.9 22.1 %slice-start.5 = ((s8[13107200]{0:T(1024)(128)(4,1)}), s8[4194304]{0:T(1024)(128)(4,1)S(1)}, s32[]{:S(2)}) async-start(s8[13107200]{0:T(1024)(128)(4,1)} %bitcast.343), calls=%async_computation.20 | async-start | bytes 8388608
  17.0 22.1 %slice-start.6 = ((s8[13107200]{0:T(1024)(128)(4,1)}), s8[4194304]{0:T(1024)(128)(4,1)S(1)}, s32[]{:S(2)}) async-start(s8[13107200]{0:T(1024)(128)(4,1)} %bitcast.343), calls=%async_computation.21 | async-start | bytes 8388608
  17.0 22.1 %slice-start.7 = ((s8[13107200]{0:T(1024)(128)(4,1)}), s8[4194304]{0:T(1024)(128)(4,1)S(1)}, s32[]{:S(2)}) async-start(s8[13107200]{0:T(1024)(128)(4,1)} %bitcast.343), calls=%async_computation.22 | async-start | bytes 8388608
  102.0 0.6 copy-start.6
  102.1 24.0 %copy-start.8 = (f32[1,1,2048]{2,1,0:T(1,128)}, f32[1,1,2048]{2,1,0:T(1,128)S(1)}, u32[]{:S(2)}) copy-start(f32[1,1,2048]{2,1,0:T(1,128)S(1)} %rsqrt.38) | copy-start | bytes 24580
  102.6 23.4 %copy-start.3 = (bf16[1,1,2048,1024]{2,3,1,0:T(8,128)(2,1)S(1)}, bf16[1,1,2048,1024]{2,3,1,0:T(8,128)(2,1)}, u32[]{:S(2)}) copy-start(bf16[1,1,2048,1024]{2,3,1,0:T(8,128)(2,1)} %get-tuple-element.10) | copy-start | bytes 12582916
  175.4 259.6 %reduce-scatter.33.cloned.1.call-start = ((), (), s32[]{:S(2)}) async-start(), calls=%async_computation.14 | async-start | bytes 13926400
  252.2 23.3 %copy-start.7 = (f32[2048]{0:T(1024)S(1)}, f32[2048]{0:T(1024)}, u32[]{:S(2)}) copy-start(f32[2048]{0:T(1024)} %copy-done.6) | copy-start | bytes 24580
  252.2 23.3 %copy-start = (bf16[1,2048,1024]{1,2,0:T(8,128)(2,1)S(1)}, bf16[1,2048,1024]{1,2,0:T(8,128)(2,1)}, u32[]{:S(2)}) copy-start(bf16[1,2048,1024]{1,2,0:T(8,128)(2,1)} %copy.1) | copy-start | bytes 12582916
  252.2 23.4 %copy-start.9 = (f32[1,1,2048]{2,1,0:T(1,128)S(1)}, f32[1,1,2048]{2,1,0:T(1,128)}, u32[]{:S(2)}) copy-start(f32[1,1,2048]{2,1,0:T(1,128)} %copy-done.8) | copy-start | bytes 24580
  280.9 2.0 copy-start.4
  302.7 186.0 %reduce-scatter.27.cloned.1.call-start = ((), (), s32[]{:S(2)}) async-start(), calls=%async_computation.11 | async-start | bytes 13926400
  328.8 21.1 %copy-start.11 = (f32[2048]{0:T(1024)S(1)}, f32[2048]{0:T(1024)}, u32[]{:S(2)}) copy-start(f32[2048]{0:T(1024)} %copy-done.10) | copy-start | bytes 24580
  328.8 252.4 %reduce-scatter.29.cloned.1.call-start = ((), (), s32[]{:S(2)}) async-start(), calls=%async_computation.12 | async-start | bytes 13926400
  328.8 21.0 %copy-start.5 = (bf16[1,2048,1024]{1,2,0:T(8,128)(2,1)S(1)}, bf16[1,2048,1024]{1,2,0:T(8,128)(2,1)}, u32[]{:S(2)}) copy-start(bf16[1,2048,1024]{1,2,0:T(8,128)(2,1)} %copy) | copy-start | bytes 12582916
  374.8 298.9 %reduce-scatter.23.cloned.1.call-start = ((), (), s32[]{:S(2)}) async-start(), calls=%async_computation.9 | async-start | bytes 13926400
  397.0 369.8 %reduce-scatter.25.cloned.1.call-start = ((), (), s32[]{:S(2)}) async-start(), calls=%async_computation.10 | async-start | bytes 13926400
  431.9 0.7 copy-start.12
  432.0 468.2 %all-gather.14.cloned.1.call-start = ((), (), s32[]{:S(2)}) async-start(), calls=%async_computation.8 | async-start | bytes 13926400 | tf_op jit(solution)/reshape | solution.py:58
  809.1 180.3 %all-gather.10.cloned.1.call-start = ((), (), s32[]{:S(2)}) async-start(), calls=%async_computation.6 | async-start | bytes 13926400 | tf_op jit(solution)/reshape | solution.py:58
  814.3 264.4 %all-gather.12.cloned.1.call-start = ((), (), s32[]{:S(2)}) async-start(), calls=%async_computation.7 | async-start | bytes 13926400 | tf_op jit(solution)/reshape | solution.py:58
  1078.7 12.7 %copy-start.2 = (bf16[1,2,1024,3200]{3,2,1,0:T(8,128)(2,1)S(1)}, bf16[1,2,1024,3200]{3,2,1,0:T(8,128)(2,1)}, u32[]{:S(2)}) copy-start(bf16[1,2,1024,3200]{3,2,1,0:T(8,128)(2,1)} %all-gather.12.cloned.1.call-done) | copy-start | bytes 39321604
  1078.7 19.4 %slice-start = ((s8[13107200]{0:T(1024)(128)(4,1)}), s8[4194304]{0:T(1024)(128)(4,1)S(1)}, s32[]{:S(2)}) async-start(s8[13107200]{0:T(1024)(128)(4,1)} %bitcast.336), calls=%async_computation.15 | async-start | bytes 8388608
  1078.7 20.5 %slice-start.1 = ((s8[13107200]{0:T(1024)(128)(4,1)}), s8[4194304]{0:T(1024)(128)(4,1)S(1)}, s32[]{:S(2)}) async-start(s8[13107200]{0:T(1024)(128)(4,1)} %bitcast.336), calls=%async_computation.16 | async-start | bytes 8388608
  1091.4 9.1 slice-start.2
  1091.4 9.1 slice-start.3
Sparse Core Ops, SparseCore 0:
  175.6 93.1 reduce-scatter.30
  302.8 93.1 reduce-scatter.32
  399.3 89.3 reduce-scatter.26
  491.8 89.3 reduce-scatter.28
  584.3 89.3 reduce-scatter.22
  677.4 89.3 reduce-scatter.24
  809.3 90.8 all-gather.13
  902.7 86.6 all-gather.9
  992.0 86.6 all-gather.11
where the time goes:
time: 1120 us; the launch traced here: 1110 us
  waiting for transfers between devices  585 us (52%)
  matrix products  350 us (31%)
  other arithmetic  83.7 us (7%)
  local copies, waits for them, and re-layouts  43.6 us (4%)
  blocking collectives  32.4 us (3%)
  between operations  17.8 us (2%)
    unnamed x15, waiting for transfers between devices  325 us
    reshape x3, waiting for transfers between devices, step(): t.reshape(-1, *t.shape[2:])  259 us
    dot_general x5, matrix products, layer(): gate = jnp.dot(a, w['w_gate'], preferred_element_type=jnp.float32)  126 us
    dot_general x5, matrix products, matmul(): jnp.dot(a, w, preferred_element_type=jnp.float32).astype(jnp.bfloat16)  112 us
    dot_general x5, matrix products, layer(): up = jnp.dot(a, w['w_up'], preferred_element_type=jnp.float32)  112 us
    unnamed x5, other arithmetic  55.1 us
    unnamed x47, local copies, waits for them, and re-layouts  43 us
    reduce_sum x1, blocking collectives, of_a_group(): jnp.sum(g * g)  32.4 us
  transfers between devices with their start and end apart: 9, of which 7 were waited for; matrix products, arithmetic and copies ran while one was open for 24% of the time, Pallas kernels for 0%

commit v1 on v0

v1 whole, which is shorter than its diff:
```python
import functools

import jax
import jax.numpy as jnp
from jax import lax
from jax.experimental import pallas as pl
from jax.experimental.pallas import tpu as pltpu
from jax.sharding import PartitionSpec as P

MESH = pl.DeviceIdType.MESH
ANY = pl.BlockSpec(memory_space=pl.ANY)
VMEM_LIMIT = 62 * 1024 * 1024
F32, BF16 = jnp.float32, jnp.bfloat16
SIDE = 4


def dot(a, b, contract):
    return lax.dot_general(a, b, (contract, ((), ())), preferred_element_type=F32)


def nn(a, b):
    return dot(a, b, ((1,), (0,)))


def nt(a, b):
    return dot(a, b, ((1,), (1,)))


def tn(a, b):
    return dot(a, b, ((0,), (0,)))


def normed(h):
    wide = h.astype(F32)
    scale = lax.rsqrt(jnp.mean(wide**2, -1, keepdims=True) + 1e-6)
    return (wide * scale).astype(BF16)


def norm_back(h, da):
    wide, da = h.astype(F32), da.astype(F32)
    scale = lax.rsqrt(jnp.mean(wide**2, -1, keepdims=True) + 1e-6)
    by_mean = jnp.sum(da * wide, -1, keepdims=True) * (-0.5 * scale * scale * scale)
    return (da * scale + wide * (by_mean * (2.0 / h.shape[-1]))).astype(BF16)


def columns(total, step):
    return [(at, min(step, total - at)) for at in range(0, total, step)]


def over_columns(total, step, body):
    whole = total // step

    def one(j, _):
        body(pl.multiple_of(j * step, step), step)
        return 0

    lax.fori_loop(0, whole, one, 0)
    if total % step:
        body(whole * step, total % step)


class Work:
    def __init__(self, grid, ins, outs, body, flops):
        self.grid, self.ins, self.outs, self.body, self.flops = grid, ins, outs, body, flops


def once(shape, index):
    return pl.BlockSpec(shape, index, pipeline_mode=pl.Buffered(1))


def gate_up(a, wg, wu, n, rows):
    t, d = a.shape
    ff = wg.shape[2]

    def body(a, wg, wu, gate, up, act):
        def piece(at, size):
            cols = pl.ds(at, size)
            g, u = nn(a[...], wg[:, cols]), nn(a[...], wu[:, cols])
            gate[:, cols] = g
            up[:, cols] = u
            act[:, cols] = (g * jax.nn.sigmoid(g) * u).astype(BF16)

        over_columns(ff, 512, piece)

    row = lambda width: pl.BlockSpec((rows, width), lambda i: (i, 0))
    weight = once((None, d, ff), lambda i: (n, 0, 0))
    return Work(
        (t // rows,),
        [(a, row(d)), (wg, weight), (wu, weight)],
        [((t, ff), F32, row(ff)), ((t, ff), F32, row(ff)), ((t, ff), BF16, row(ff))],
        body,
        4 * t * d * ff,
    )


def down(act, wd, x, n, rows):
    t, ff = act.shape
    d = wd.shape[2]

    def body(act, wd, x, h, a):
        for at, size in columns(d, 512):
            h[:, at : at + size] = x[:, at : at + size] + nn(act[...], wd[:, at : at + size]).astype(BF16)
        a[...] = normed(h[...])

    row = lambda width: pl.BlockSpec((rows, width), lambda i: (i, 0))
    return Work(
        (t // rows,),
        [(act, row(ff)), (wd, once((None, ff, d), lambda i: (n, 0, 0))), (x, row(d))],
        [((t, d), BF16, row(d)), ((t, d), BF16, row(d))],
        body,
        2 * t * d * ff,
    )


def silu_back(g, u, dact):
    s = jax.nn.sigmoid(g)
    silu = g * s
    return (dact * u * (s + silu * (1.0 - s))).astype(BF16), (dact * silu).astype(BF16)


def last_layer(a, dy, wg, wu, wd, n, rows):
    t, d = a.shape
    ff = wg.shape[2]

    def body(a, dy, wg, wu, wd, act, dgu):
        def piece(at, size):
            cols = pl.ds(at, size)
            g, u = nn(a[...], wg[:, cols]), nn(a[...], wu[:, cols])
            dact = nt(dy[...], wd[cols, :]).astype(BF16).astype(F32)
            s = jax.nn.sigmoid(g)
            silu = g * s
            act[:, cols] = (silu * u).astype(BF16)
            dgu[0, :, cols] = (dact * u * (s + silu * (1.0 - s))).astype(BF16)
            dgu[1, :, cols] = (dact * silu).astype(BF16)

        over_columns(ff, 512, piece)

    row = lambda width: pl.BlockSpec((rows, width), lambda i: (i, 0))
    weight = once((None, d, ff), lambda i: (n, 0, 0))
    return Work(
        (t // rows,),
        [(a, row(d)), (dy, row(d)), (wg, weight), (wu, weight), (wd, once((None, ff, d), lambda i: (n, 0, 0)))],
        [((t, ff), BF16, row(ff)), ((2, t, ff), BF16, pl.BlockSpec((2, rows, ff), lambda i: (0, i, 0)))],
        body,
        6 * t * d * ff,
    )


def hidden_back(dh, wd, gate, up, n, rows):
    t, d = dh.shape
    ff = wd.shape[1]

    def body(dh, wd, gate, up, dgu):
        def piece(at, size):
            cols = pl.ds(at, size)
            dact = nt(dh[...], wd[cols, :]).astype(BF16).astype(F32)
            dgu[0, :, cols], dgu[1, :, cols] = silu_back(gate[:, cols], up[:, cols], dact)

        over_columns(ff, 512, piece)

    row = lambda width: pl.BlockSpec((rows, width), lambda i: (i, 0))
    return Work(
        (t // rows,),
        [(dh, row(d)), (wd, once((None, ff, d), lambda i: (n, 0, 0))), (gate, row(ff)), (up, row(ff))],
        [((2, t, ff), BF16, pl.BlockSpec((2, rows, ff), lambda i: (0, i, 0)))],
        body,
        2 * t * d * ff,
    )


def input_back(dgu, wg, wu, h, dy, n, rows):
    _, t, ff = dgu.shape
    d = wg.shape[1]

    def body(dgu, wg, wu, h, dy, out, da):
        for at, size in columns(d, 512):
            cols = slice(at, at + size)
            da[:, cols] = nt(dgu[0], wg[cols, :]).astype(BF16) + nt(dgu[1], wu[cols, :]).astype(BF16)
        out[...] = dy[...] + norm_back(h[...], da[...])

    row = lambda width: pl.BlockSpec((rows, width), lambda i: (i, 0))
    weight = once((None, d, ff), lambda i: (n, 0, 0))
    return Work(
        (t // rows,),
        [(dgu, pl.BlockSpec((2, rows, ff), lambda i: (0, i, 0))), (wg, weight), (wu, weight), (h, row(d)), (dy, row(d))],
        [((t, d), BF16, row(d)), ((t, d), BF16, row(d))],
        body,
        4 * t * d * ff,
    )


def by_down(act, dh, tile):
    t, ff = act.shape
    d = dh.shape[1]

    def body(act, dh, out):
        out[...] = tn(act[...], dh[...]).astype(BF16)

    return Work(
        (ff // tile,),
        [(act, pl.BlockSpec((t, tile), lambda i: (0, i))), (dh, once((t, d), lambda i: (0, 0)))],
        [((ff, d), BF16, pl.BlockSpec((tile, d), lambda i: (i, 0)))],
        body,
        2 * t * d * ff,
    )


def by_gate_up(a, dgu, tile):
    t, d = a.shape
    ff = dgu.shape[2]
    tiles = ff // tile

    def body(a, dgu, out):
        out[...] = tn(a[...], dgu[...]).astype(BF16)

    return Work(
        (2 * tiles,),
        [(a, once((t, d), lambda i: (0, 0))), (dgu, pl.BlockSpec((None, t, tile), lambda i: (i // tiles, 0, i % tiles)))],
        [((2, d, ff), BF16, pl.BlockSpec((None, d, tile), lambda i: (i // tiles, 0, i % tiles)))],
        body,
        4 * t * d * ff,
    )


class Split:
    def __init__(self, rows, width, by_rows):
        self.rows, self.width, self.by_rows = rows, width, by_rows
        first = (width // 128 + 1) // 2 * 128
        self.colours = [(0, first), (first, width - first)]

    def part(self, colour, half):
        at, size = self.colours[colour]
        if self.by_rows:
            return pl.ds(half * (self.rows // 2), self.rows // 2), pl.ds(at, size)
        return pl.ds(0, self.rows), pl.ds(at + half * (size // 2), size // 2)

    def piece(self, colour):
        size = self.colours[colour][1]
        return (self.rows // 2, size) if self.by_rows else (self.rows, size // 2)

    def join(self, colours):
        along = 0 if self.by_rows else 1
        return jnp.concatenate([jnp.concatenate([c[0], c[1]], along) for c in colours], 1)


def position():
    me = lax.axis_index("dp")
    return lax.div(me, SIDE), lax.rem(me, SIDE)


def along(axis, at):
    x, y = position()
    return at * SIDE + y if axis == 0 else x * SIDE + at


def neighbours():
    x, y = position()
    for axis, here in ((0, x), (1, y)):
        for step in (1, SIDE - 1):
            yield along(axis, lax.rem(here + step, SIDE))


class Ring:
    def __init__(self, axis, source, own, scratch):
        self.axis, self.source, self.own = axis, source, own
        self.far, self.near, self.sums, self.terms, self.mine, self.send, self.recv, self.load = scratch
        here = position()[axis]
        self.here, self.right, self.left = here, lax.rem(here + 1, SIDE), lax.rem(here + SIDE - 1, SIDE)
        self.across = lax.rem(here + 2, SIDE)

    def message(self, i):
        src, dst = (
            (lambda: self.source(0, self.across), self.far.at[0]),
            (lambda: self.source(1, self.across), self.far.at[1]),
            (lambda: self.source(1, self.right), self.near.at[1]),
            (lambda: self.source(0, self.left), self.near.at[0]),
            (lambda: self.far.at[0], self.sums.at[0]),
            (lambda: self.far.at[1], self.sums.at[1]),
        )[i]
        to = self.right if i % 2 == 0 else self.left
        return pltpu.make_async_remote_copy(
            src_ref=src(),
            dst_ref=dst,
            send_sem=self.send.at[i],
            recv_sem=self.recv.at[i],
            device_id={"dp": along(self.axis, to)},
            device_id_type=MESH,
        )

    def local(self, i):
        src, dst = (
            (lambda: self.source(0, self.right), self.terms.at[0]),
            (lambda: self.source(1, self.left), self.terms.at[1]),
            (lambda: self.own(0), self.mine.at[0]),
            (lambda: self.own(1), self.mine.at[1]),
        )[i]
        return pltpu.make_async_copy(src(), dst, self.load.at[i])

    def start(self, first):
        for i in (0, 1) if first else (2, 3):
            self.message(i).start()

    def start_loads(self):
        for i in range(4):
            self.local(i).start()

    def relay(self):
        for half in (0, 1):
            self.local(half).wait()
            self.message(half).wait()
            self.far[half] = (self.far[half].astype(F32) + self.terms[half].astype(F32)).astype(BF16)
            self.message(4 + half).start()

    def finish(self, take):
        for half in (0, 1):
            self.local(2 + half).wait()
        for i in (2, 3, 4, 5):
            self.message(i).wait()
        for half in (0, 1):
            take(half)


def ring_scratch(shape, own_type):
    return [
        pltpu.VMEM((2, *shape), BF16),
        pltpu.VMEM((2, *shape), BF16),
        pltpu.VMEM((2, *shape), BF16),
        pltpu.VMEM((2, *shape), BF16),
        pltpu.VMEM((2, *shape), own_type),
        pltpu.SemaphoreType.DMA((6,)),
        pltpu.SemaphoreType.DMA((6,)),
        pltpu.SemaphoreType.DMA((4,)),
    ]


RING_SCRATCH = 8


class First:
    def __init__(self, term, split):
        self.term, self.split = term, split

    def ins(self):
        return [(self.term, ANY)]

    def outs(self):
        made = []
        for colour in (0, 1):
            piece = self.split.piece(colour)
            for shape, kind in (((2, SIDE, *piece), BF16), ((2, *piece), F32)):
                made.append((shape, kind, pl.BlockSpec(shape, lambda i, n=len(shape): (0,) * n)))
        return made

    def scratch(self):
        return [s for colour in (0, 1) for s in ring_scratch((SIDE, *self.split.piece(colour)), BF16)]

    def rings(self, ins, outs, scratch):
        (term,) = ins
        made = []
        for colour in (0, 1):

            def source(half, at, colour=colour):
                rows, cols = self.split.part(colour, half)
                return term.at[at, :, rows, cols] if colour == 0 else term.at[:, at, rows, cols]

            axis = colour
            ring = Ring(axis, source, lambda half, s=source, axis=axis: s(half, position()[axis]), scratch[colour * RING_SCRATCH :][:RING_SCRATCH])
            made.append((ring, functools.partial(self.take, ring, outs[2 * colour], outs[2 * colour + 1], 1 - axis)))
        return made

    def take(self, ring, out, own, other, half):
        total = lambda at: ring.mine[half, at].astype(F32) + ring.sums[half, at].astype(F32) + ring.near[half, at].astype(F32)
        for at in range(SIDE):
            out[half, at] = total(at).astype(BF16)
        own[half] = total(position()[other])


class Second:
    def __init__(self, parts, split):
        self.parts, self.split = parts, split

    def ins(self):
        return [(p, ANY) for p in self.parts]

    def outs(self):
        shapes = [(2, *self.split.piece(colour)) for colour in (0, 1)]
        return [(shape, BF16, pl.BlockSpec(shape, lambda i: (0, 0, 0))) for shape in shapes]

    def scratch(self):
        return [s for colour in (0, 1) for s in ring_scratch(self.split.piece(colour), F32)]

    def rings(self, ins, outs, scratch):
        made = []
        for colour in (0, 1):
            part, own = ins[2 * colour : 2 * colour + 2]
            ring = Ring(
                1 - colour,
                lambda half, at, part=part: part.at[half, at],
                lambda half, own=own: own.at[half],
                scratch[colour * RING_SCRATCH :][:RING_SCRATCH],
            )
            made.append((ring, functools.partial(self.take, ring, outs[colour])))
        return made

    def take(self, ring, out, half):
        out[half] = (ring.mine[half] + ring.sums[half].astype(F32) + ring.near[half].astype(F32)).astype(BF16)


def run(work=None, first=None, second=None, name=None, number=None, relay=(0.3, 0.5)):
    parts = [p for p in (second, first) if p is not None]
    grid = work.grid if work else (1,)
    steps = grid[0]
    groups = ([work] if work else []) + parts
    ins = [list(work.ins)] if work else []
    ins += [p.ins() for p in parts]
    outs = [list(work.outs)] if work else []
    outs += [p.outs() for p in parts]
    scratch = [p.scratch() for p in parts]

    def cut(refs, sizes):
        made = []
        for size in sizes:
            made.append(refs[:size])
            refs = refs[size:]
        return made

    n_in, n_out = sum(map(len, ins)), sum(map(len, outs))

    def kernel(*refs):
        in_refs = cut(refs[:n_in], [len(i) for i in ins])
        out_refs = cut(refs[n_in : n_in + n_out], [len(o) for o in outs])
        scratch_refs = cut(refs[n_in + n_out :], [len(s) for s in scratch])
        step = pl.program_id(0)
        skip = 1 if work else 0
        rings = [p.rings(in_refs[skip + i], out_refs[skip + i], scratch_refs[i]) for i, p in enumerate(parts)]
        if parts:

            @pl.when(step == 0)
            def _():
                barrier = pltpu.get_barrier_semaphore()
                for device in neighbours():
                    pl.semaphore_signal(barrier, inc=1, device_id={"dp": device}, device_id_type=MESH)
                pl.semaphore_wait(barrier, 4)
                for first_ones in (True, False):
                    for group in rings:
                        for ring, _ in group:
                            ring.start(first_ones)
                for group in rings:
                    for ring, _ in group:
                        ring.start_loads()

            for i, group in enumerate(rings):
                at = int(steps * (relay[i] if len(rings) == 2 else relay[1]))

                @pl.when(step == at)
                def _():
                    for ring, _ in group:
                        ring.relay()

        if work:
            work.body(*in_refs[0], *out_refs[0])
        if parts:

            @pl.when(step == steps - 1)
            def _():
                for group in rings:
                    for ring, take in group:
                        ring.finish(take)

    made = pl.pallas_call(
        kernel,
        out_shape=[jax.ShapeDtypeStruct(shape, kind) for group in outs for shape, kind, _ in group],
        grid_spec=pltpu.PrefetchScalarGridSpec(
            num_scalar_prefetch=0,
            grid=grid,
            in_specs=[spec for group in ins for _, spec in group],
            out_specs=[spec for group in outs for _, _, spec in group],
            scratch_shapes=[s for group in scratch for s in group],
        ),
        compiler_params=pltpu.CompilerParams(
            dimension_semantics=("arbitrary",),
            vmem_limit_bytes=VMEM_LIMIT,
            **(dict(collective_id=number, has_side_effects=True) if parts else {}),
        ),
        cost_estimate=pl.CostEstimate(flops=work.flops if work else 1000, bytes_accessed=1 << 24, transcendentals=0),
        name=name,
    )(*[a for group in ins for a, _ in group])
    return cut(made, [len(o) for o in outs])


def everywhere(own, number, members):
    def kernel(own, out, send, recv, load):
        me = lax.axis_index("dp")
        barrier = pltpu.get_barrier_semaphore()
        peers = [lax.rem(me + i, members) for i in range(1, members)]
        for peer in peers:
            pl.semaphore_signal(barrier, inc=1, device_id={"dp": peer}, device_id_type=MESH)
        pl.semaphore_wait(barrier, members - 1)
        keep = pltpu.make_async_copy(own, out.at[me], load)
        keep.start()

        def copy(i, slot):
            return pltpu.make_async_remote_copy(
                src_ref=own, dst_ref=out.at[slot], send_sem=send.at[i], recv_sem=recv.at[i], device_id={"dp": peers[i]}, device_id_type=MESH
            )

        for i in range(members - 1):
            copy(i, me).start()
        keep.wait()
        for i in range(members - 1):
            copy(i, me).wait_send()
            copy(i, lax.rem(me + members - 1 - i, members)).wait_recv()

    return pl.pallas_call(
        kernel,
        out_shape=jax.ShapeDtypeStruct((members, *own.shape), own.dtype),
        in_specs=[ANY],
        out_specs=pl.BlockSpec(memory_space=pl.ANY),
        scratch_shapes=[pltpu.SemaphoreType.DMA((members - 1,)), pltpu.SemaphoreType.DMA((members - 1,)), pltpu.SemaphoreType.DMA],
        compiler_params=pltpu.CompilerParams(collective_id=number, has_side_effects=True),
        name="everywhere",
    )(own)


def adamw(w, m, v, g):
    m = 0.9 * m + 0.1 * g
    v = 0.95 * v + 0.05 * g * g
    step = m * lax.rsqrt(v + 1e-8) + 0.1 * w
    return (w - 0.02 * step).astype(BF16), m, v


def solution(mesh):
    members = mesh.shape["dp"]

    def step(x, dy, wg, wu, wd, *moments):
        x, dy = x[0], dy[0]
        d, ff = wg.shape[1:]
        wide, tall = Split(d // members, ff, True), Split(ff // members, d, False)
        square = lambda t: t.reshape(SIDE, SIDE, t.shape[0] // members, t.shape[1])

        a0 = normed(x)
        [[gate0, up0, act0]] = run(gate_up(a0, wg, wu, 0, 256), name="gate_up_0")
        [[h1, a1]] = run(down(act0, wd, x, 0, 512), name="down_0")
        [[act1, dgu1]] = run(last_layer(a1, dy, wg, wu, wd, 1, 256), name="layer_1")
        [[d1]] = run(by_down(act1, dy, 640), name="by_down_1")
        [[gu1], d1_half] = run(by_gate_up(a1, dgu1, 640), First(square(d1), tall), name="by_gate_up_1", number=1)
        [[dh1, _], d1_sum, g1_half] = run(
            input_back(dgu1, wg, wu, h1, dy, 1, 256), First(square(gu1[0]), wide), Second(d1_half, tall), name="input_back_1", number=2
        )
        [[dgu0], g1_sum, u1_half] = run(
            hidden_back(dh1, wd, gate0, up0, 0, 256), First(square(gu1[1]), wide), Second(g1_half, wide), name="hidden_back_0", number=3
        )
        [[d0], u1_sum] = run(by_down(act0, dh1, 640), None, Second(u1_half, wide), name="by_down_0", number=4)
        [[gu0], d0_half] = run(by_gate_up(a0, dgu0, 640), First(square(d0), tall), name="by_gate_up_0", number=5)
        d0_sum, g0_half = run(None, First(square(gu0[0]), wide), Second(d0_half, tall), name="sum_gate_0", number=6)
        g0_sum, u0_half = run(None, First(square(gu0[1]), wide), Second(g0_half, wide), name="sum_up_0", number=7)
        [u0_sum] = run(None, None, Second(u0_half, wide), name="sum_end", number=8)

        g = [
            jnp.stack([split.join(one) for one in sums]).astype(F32)
            for split, sums in ((wide, (g0_sum, g1_sum)), (wide, (u0_sum, u1_sum)), (tall, (d0_sum, d1_sum)))
        ]
        squares = jnp.broadcast_to(sum(jnp.sum(one * one) for one in g), (8, 128))
        squares = jnp.sum(everywhere(squares, 9, members)[:, 0, 0])
        count = sum(w.size for w in (wg, wu, wd))
        factor = jnp.minimum(1.0, 0.5 * lax.rsqrt(squares / count + 1e-30))
        me = lax.axis_index("dp")
        new = []
        for w, m, v, one in zip((wg, wu, wd), moments[:3], moments[3:], g, strict=True):
            rows = w.shape[1] // members
            mine = lax.dynamic_slice_in_dim(w, me * rows, rows, 1).astype(F32)
            w, m, v = adamw(mine, m, v, one * factor)
            new.append((lax.all_gather(w, "dp", axis=1, tiled=True), m, v))
        return tuple(one[which] for which in range(3) for one in new)

    parts, whole, moment, out = P(("rep", "dp"), None, None), P(None, None, None), P(None, "dp", None), P("rep", "dp", None)
    return jax.shard_map(
        step,
        mesh=mesh,
        in_specs=(parts,) * 2 + (whole,) * 3 + (moment,) * 6,
        out_specs=(P("rep", None, None),) * 3 + (out,) * 6,
        check_vma=False,
    )
```

time: 1120 us -> 816 us (0.73)
  Pallas kernels: 0 us -> 456 us
  matrix products: 350 us -> 0 us
  waiting for transfers between devices: 585 us -> 262 us
  other arithmetic: 83.7 us -> 24.3 us
  blocking collectives: 32.4 us -> 0 us
    pallas_call x0 -> x13, Pallas kernels: none -> 456 us  [the longest x12 450 us: run(): pl.pallas_call(kernel, out_shape=[jax.ShapeDtypeStruct(shape, kind) for g...]
    dot_general x15 -> x0, matrix products: 350 us -> none  [the longest x5 126 us: layer(): gate = jnp.dot(a, w['w_gate'], preferred_element_type=jnp.float32)]
    unnamed x15 -> x3, waiting for transfers between devices: 325 us -> 0.16 us
    all_gather x0 -> x3, waiting for transfers between devices: none -> 262 us  [step(): new.append((lax.all_gather(w, 'dp', axis=1, tiled=True), m, v))]
    reshape x3 -> x0, waiting for transfers between devices: 259 us -> none  [step(): t.reshape(-1, *t.shape[2:])]
    unnamed x5 -> x1, other arithmetic: 55.1 us -> 0.01 us
    reduce_sum x1 -> x0, blocking collectives: 32.4 us -> none  [of_a_group(): jnp.sum(g * g)]
    slice x0 -> x2, local copies, waits for them, and re-layouts: none -> 20.8 us  [the longest x1 10.4 us: step(): gu0[1]]
  transfers between devices with their start and end apart: 9 -> 3, of which waited for: 7 -> 3; matrix products, arithmetic and copies ran while one was open for 24% -> 1% of each run, Pallas kernels for 0% -> 0%
where the time goes in v1:
time: 816 us; the launch traced here: 811 us
  Pallas kernels  456 us (56%)
  waiting for transfers between devices  262 us (32%)
  local copies, waits for them, and re-layouts  51.3 us (6%)
  other arithmetic  24.3 us (3%)
  between operations  17.2 us (2%)
    pallas_call x12, Pallas kernels, run(): pl.pallas_call(kernel, out_shape=[jax.ShapeDtypeStruct(shape, kind) for g...  450 us
    all_gather x3, waiting for transfers between devices, step(): new.append((lax.all_gather(w, 'dp', axis=1, tiled=True), m, v))  262 us
    unnamed x37, local copies, waits for them, and re-layouts  27.8 us
  transfers between devices with their start and end apart: 3, of which 3 were waited for; matrix products, arithmetic and copies ran while one was open for 1% of the time, Pallas kernels for 0%

profile of v1, /device:TPU:97, one launch (start us, length us, event | category | flops | bytes accessed | tf_op | source)
XLA Modules:
  0.0 811.4 jit_solution(16434464579702430617)
XLA Ops:
  7.2 0.1 all-gather.8.cloned.1.call-start
  7.3 0.0 copy-start
  7.3 3.2 fusion
  10.5 0.2 copy-done
  10.7 2.7 fusion.1.refs_0_
  13.5 46.1 %gate_up_0.1 = (f32[2048,3200]{1,0:T(8,128)}, f32[2048,3200]{1,0:T(8,128)}, bf16[2048,3200]{1,0:T(8,128)(2,1)}) custom-call(bf16[2048,1024]{1,0:T(8,128)(2,1)} %fusion.1.refs_0_, bf16[2,1024,3200]{2,1,0:T(8,128)(2,1)} %refs_1_.6, bf16[2,1024,3200]{2,1,0:T(8,128)(2,1)} %refs_2_.5), custom_call_target="tpu_custom_call" | custom-call | flops 26843545600 | bytes 16777216 | tf_op jit(solution)/shard_map/gate_up_0/pallas_call | solution.py:470
  59.5 21.7 %down_0.1 = (bf16[2048,1024]{1,0:T(8,128)(2,1)}, bf16[2048,1024]{1,0:T(8,128)(2,1)}) custom-call(bf16[2048,3200]{1,0:T(8,128)(2,1)} %get-tuple-element.57.refs_0_, bf16[2,3200,1024]{2,1,0:T(8,128)(2,1)} %refs_1_.7, bf16[2048,1024]{1,0:T(8,128)(2,1)} %bitcast.73), custom_call_target="tpu_custom_call" | custom-call | flops 13421772800 | bytes 16777216 | tf_op jit(solution)/shard_map/down_0/pallas_call | solution.py:470
  81.3 65.3 %layer_1.1 = (bf16[2048,3200]{1,0:T(8,128)(2,1)}, bf16[2,2048,3200]{2,1,0:T(8,128)(2,1)}) custom-call(bf16[2048,1024]{1,0:T(8,128)(2,1)} %get-tuple-element.58.refs_0_, bf16[2048,1024]{1,0:T(8,128)(2,1)} %bitcast.77, bf16[2,1024,3200]{2,1,0:T(8,128)(2,1)} %refs_1_.6, bf16[2,1024,3200]{2,1,0:T(8,128)(2,1)} %refs_2_.5, bf16[2,3200,1024]{2,1,0:T(8,128)(2,1)} %refs_1_.7), custom_call_target="tpu_custom_call" | custom-call | flops 40265318400 | bytes 16777216 | tf_op jit(solution)/shard_map/layer_1/pallas_call | solution.py:470
  146.5 18.6 %by_down_1.1 = bf16[3200,1024]{1,0:T(8,128)(2,1)} custom-call(bf16[2048,3200]{1,0:T(8,128)(2,1)} %get-tuple-element.61.refs_0_, bf16[2048,1024]{1,0:T(8,128)(2,1)} %bitcast.78), custom_call_target="tpu_custom_call" | custom-call | flops 13421772800 | bytes 16777216 | tf_op jit(solution)/shard_map/by_down_1/pallas_call | solution.py:470
  165.1 47.3 %by_gate_up_1.1 = (bf16[2,1024,3200]{2,1,0:T(8,128)(2,1)}, bf16[2,4,200,256]{3,2,1,0:T(8,128)(2,1)}, f32[2,200,256]{2,1,0:T(8,128)}, bf16[2,4,200,256]{3,2,1,0:T(8,128)(2,1)}, f32[2,200,256]{2,1,0:T(8,128)}) custom-call(bf16[2048,1024]{1,0:T(8,128)(2,1)} %get-tuple-element.58.refs_0_, bf16[2,2048,3200]{2,1,0:T(8,128)(2,1)} %get-tuple-element.59.refs_1_.refs_0_, ...), custom_call_target="tpu_custom_call" | custom-call | flops 26843545600 | bytes 16777216 | tf_op jit(solution)/shard_map/by_gate_up_1/pallas_call | solution.py:470
  212.5 10.4 %fusion.30 = (bf16[1,1024,3200]{2,1,0:T(8,128)(2,1)}, bf16[1,1024,3200]{2,1,0:T(8,128)(2,1)}) fusion(bf16[2,1024,3200]{2,1,0:T(8,128)(2,1)} %get-tuple-element.66), kind=kLoop, calls=%fused_computation.76 | loop fusion | bytes 26214400 | tf_op jit(solution)/shard_map/slice | solution.py:551
  222.9 57.1 %input_back_1.1 = (bf16[2048,1024]{1,0:T(8,128)(2,1)}, bf16[2048,1024]{1,0:T(8,128)(2,1)}, bf16[2,200,256]{2,1,0:T(8,128)(2,1)}, bf16[2,200,256]{2,1,0:T(8,128)(...) custom-call(bf16[2,2048,3200]{2,1,0:T(8,128)(2,1)} %get-tuple-elemen, ...), custom_call_target="tpu_custom_call" | custom-call | flops 26843545600 | bytes 16777216 | tf_op jit(solution)/shard_map/input_back_1/pallas_call | solution.py:470
  279.9 45.5 %hidden_back_0.1 = (bf16[2,2048,3200]{2,1,0:T(8,128)(2,1)}, bf16[2,32,1664]{2,1,0:T(8,128)(2,1)}, bf16[2,32,1536]{2,1,0:T(8,128)(2,1)}, bf16[2,4,32,1664]{3,2,1,...) custom-call(bf16[2048,1024]{1,0:T(8,128)(2,1)} %get-tuple-element.67.refs_0_.refs_, ...), custom_call_target="tpu_custom_call" | custom-call | flops 13421772800 | bytes 16777216 | tf_op jit(solution)/shard_map/hidden_back_0/pallas_call | solution.py:470
  325.4 21.9 %by_down_0.1 = (bf16[3200,1024]{1,0:T(8,128)(2,1)}, bf16[2,32,1664]{2,1,0:T(8,128)(2,1)}, bf16[2,32,1536]{2,1,0:T(8,128)(2,1)}) custom-call(bf16[2048,3200]{1,0:T(8,128)(2,1)} %get-tuple-element.57.refs_0_, bf16[2048,1024]{1,0:T(8,128)(2,1)} %get-tuple-element.67.refs_0_.refs_1_, bf16[2,4,32,1664]{3,2,1,0:T(8,128)(2,1)} %get-tuple-element.75.refs_2_, ...), custom_call_target="tpu_custom_call" | custom-call | flops 13421772800 | bytes 16777216 | tf_op jit(solution)/shard_map/by_down_0/pallas_call | solution.py:470
  347.3 42.6 %by_gate_up_0.1 = (bf16[2,1024,3200]{2,1,0:T(8,128)(2,1)}, bf16[2,4,200,256]{3,2,1,0:T(8,128)(2,1)}, f32[2,200,256]{2,1,0:T(8,128)}, bf16[2,4,200,256]{3,2,1,0:T(8,128)(2,1)}, f32[2,200,256]{2,1,0:T(8,128)}) custom-call(bf16[2048,1024]{1,0:T(8,128)(2,1)} %fusion.1.refs_0_, bf16[2,2048,3200]{2,1,0:T(8,128)(2,1)} %get-tuple-element.74.refs_1_, ...), custom_call_target="tpu_custom_call" | custom-call | flops 26843545600 | bytes 16777216 | tf_op jit(solution)/shard_map/by_gate_up_0/pallas_call | solution.py:470
  389.9 10.4 %fusion.29 = (bf16[1,1024,3200]{2,1,0:T(8,128)(2,1)}, bf16[1,1024,3200]{2,1,0:T(8,128)(2,1)}) fusion(bf16[2,1024,3200]{2,1,0:T(8,128)(2,1)} %get-tuple-element.84), kind=kLoop, calls=%fused_computation.75 | loop fusion | bytes 26214400 | tf_op jit(solution)/shard_map/slice | solution.py:556
  400.3 36.8 %sum_gate_0.1 = (bf16[2,200,256]{2,1,0:T(8,128)(2,1)}, bf16[2,200,256]{2,1,0:T(8,128)(2,1)}, bf16[2,4,32,1664]{3,2,1,0:T(8,128)(2,1)}, f32[2,32,1664]{2,1,0:T(8,...) custom-call(bf16[2,4,200,256]{3,2,1,0:T(8,128)(2,1)} %get-tuple-element.80.refs_0_, ...), custom_call_target="tpu_custom_call" | custom-call | flops 1000 | bytes 16777216 | tf_op jit(solution)/shard_map/sum_gate_0/pallas_call | solution.py:470
  437.2 35.9 %sum_up_0.1 = (bf16[2,32,1664]{2,1,0:T(8,128)(2,1)}, bf16[2,32,1536]{2,1,0:T(8,128)(2,1)}, bf16[2,4,32,1664]{3,2,1,0:T(8,128)(2,1)}, f32[2,32,1664]{2,1,0:T(8,12...) custom-call(bf16[2,4,32,1664]{3,2,1,0:T(8,128)(2,1)} %get-tuple-element.85.refs_0_, ...), custom_call_target="tpu_custom_call" | custom-call | flops 1000 | bytes 16777216 | tf_op jit(solution)/shard_map/sum_up_0/pallas_call | solution.py:470
  473.0 0.0 copy-start.4
  473.1 0.0 copy-start.11
  473.1 0.0 copy-start.5
  473.1 10.8 %sum_end.1 = (bf16[2,32,1664]{2,1,0:T(8,128)(2,1)}, bf16[2,32,1536]{2,1,0:T(8,128)(2,1)}) custom-call(bf16[2,4,32,1664]{3,2,1,0:T(8,128)(2,1)} %get-tuple-element.93.refs_0_, f32[2,32,1664]{2,1,0:T(8,128)} %get-tuple-element.94.refs_1_, bf16[2,4,32,1536]{3,2,1,0:T(8,128)(2,1)} %get-tuple-element.95.refs_2_, f32[2,32,1536]{2,1,0:T(8,128)} %get-tuple-element.96.refs_3_), custom_call_target="tpu_custom_call" | custom-call | flops 1000 | bytes 16777216 | tf_op jit(solution)/shard_map/sum_end/pallas_call | solution.py:470
  483.9 0.0 copy-start.12
  483.9 0.0 copy-start.3
  483.9 0.0 copy-start.10
  484.0 0.0 copy-start.8
  484.0 0.0 copy-start.9
  484.0 1.0 slice_bitcast_fusion.3
  485.0 1.0 slice_bitcast_fusion.19
  486.0 0.0 copy-done.4
  486.0 0.0 copy-start.6
  486.0 0.0 copy-start.7
  486.1 0.0 copy-done.5
  486.2 0.0 copy-done.10
  486.3 0.7 copy-done.6
  486.9 0.1 copy-done.7
  487.1 1.0 fusion.13
  488.2 0.1 maximum_bitcast_fusion.2
  488.2 1.0 fusion.12
  489.3 0.1 maximum_bitcast_fusion
  489.3 1.0 fusion.11
  492.3 0.6 broadcast_in_dim.4.own
  492.9 6.9 everywhere.1
  499.8 1.5 slice_reduce_fusion
  501.9 4.8 fusion.19
  506.7 0.1 all-gather.8.cloned.1.call-update
  506.7 0.1 all-gather.6.cloned.1.call-start
  506.8 0.0 copy-start.2
  506.8 4.7 fusion.16
  511.5 0.1 all-gather.6.cloned.1.call-update
  511.6 0.1 all-gather.4.cloned.1.call-start
  511.7 0.0 copy-done.2
  511.7 4.1 fusion.10
  515.8 0.1 all-gather.4.cloned.1.call-update
  515.9 83.4 %all-gather.8.cloned.1.call-done = bf16[2,3200,1024]{2,1,0:T(8,128)(2,1)} async-done(((bf16[2,200,1024]{2,1,0:T(8,128)(2,1)}), bf16[2,3200,1024]{2,1,0:T(8,128)(2,1)}) %all-gather.8.cloned.1.call-update) | async-done | bytes 13107216 | tf_op jit(solution)/shard_map/all_gather | solution.py:573
  599.2 89.3 %all-gather.6.cloned.1.call-done = bf16[2,1024,3200]{2,1,0:T(8,128)(2,1)} async-done(((bf16[2,64,3200]{2,1,0:T(8,128)(2,1)}), bf16[2,1024,3200]{2,1,0:T(8,128)(2,1)}) %all-gather.6.cloned.1.call-update) | async-done | bytes 13107216 | tf_op jit(solution)/shard_map/all_gather | solution.py:573
  688.5 89.3 %all-gather.4.cloned.1.call-done = bf16[2,1024,3200]{2,1,0:T(8,128)(2,1)} async-done(((bf16[2,64,3200]{2,1,0:T(8,128)(2,1)}), bf16[2,1024,3200]{2,1,0:T(8,128)(2,1)}) %all-gather.4.cloned.1.call-update) | async-done | bytes 13107216 | tf_op jit(solution)/shard_map/all_gather | solution.py:573
  777.7 12.7 %copy.23 = bf16[2,1024,3200]{2,1,0:T(8,128)(2,1)} copy(bf16[2,1024,3200]{2,1,0:T(8,128)(2,1)} %all-gather.4.cloned.1.call-done) | data formatting | bytes 26214400
  790.4 0.0 copy-done.1
  790.5 6.6 copy.24
  797.1 1.2 slice-done.1
  798.3 1.3 slice-done.2
  799.5 0.0 slice-done.3
  799.6 4.9 copy.25
  (23 shorter events, 0.3 us)
Async XLA Ops:
  7.2 592.0 %all-gather.8.cloned.1.call-start = ((), (), s32[]{:S(2)}) async-start(), calls=%async_computation.2 | async-start | bytes 13926400 | tf_op jit(solution)/shard_map/all_gather | solution.py:573
  7.3 3.5 copy-start
  473.0 12.9 %copy-start.4 = (bf16[2,32,1664]{2,1,0:T(8,128)(2,1)S(1)}, bf16[2,32,1664]{2,1,0:T(8,128)(2,1)}, u32[]{:S(2)}) copy-start(bf16[2,32,1664]{2,1,0:T(8,128)(2,1)} %get-tuple-element.99) | copy-start | bytes 638980
  473.1 13.0 %copy-start.11 = (bf16[2,32,1536]{2,1,0:T(8,128)(2,1)S(1)}, bf16[2,32,1536]{2,1,0:T(8,128)(2,1)}, u32[]{:S(2)}) copy-start(bf16[2,32,1536]{2,1,0:T(8,128)(2,1)} %get-tuple-element.100) | copy-start | bytes 589828
  473.1 13.0 %copy-start.5 = (bf16[2,32,1664]{2,1,0:T(8,128)(2,1)S(1)}, bf16[2,32,1664]{2,1,0:T(8,128)(2,1)}, u32[]{:S(2)}) copy-start(bf16[2,32,1664]{2,1,0:T(8,128)(2,1)} %get-tuple-element.89) | copy-start | bytes 638980
  483.9 2.2 copy-start.12
  483.9 2.2 copy-start.3
  483.9 2.2 copy-start.10
  484.0 2.3 copy-start.8
  484.0 2.3 copy-start.9
  486.0 0.9 copy-start.6
  486.0 1.0 copy-start.7
  506.7 181.7 %all-gather.6.cloned.1.call-start = ((), (), s32[]{:S(2)}) async-start(), calls=%async_computation.1 | async-start | bytes 13926400 | tf_op jit(solution)/shard_map/all_gather | solution.py:573
  506.8 4.9 copy-start.2
  511.6 266.1 %all-gather.4.cloned.1.call-start = ((), (), s32[]{:S(2)}) async-start(), calls=%async_computation | async-start | bytes 13926400 | tf_op jit(solution)/shard_map/all_gather | solution.py:573
  777.7 12.7 %copy-start.1 = (bf16[2,1024,3200]{2,1,0:T(8,128)(2,1)S(1)}, bf16[2,1024,3200]{2,1,0:T(8,128)(2,1)}, u32[]{:S(2)}) copy-start(bf16[2,1024,3200]{2,1,0:T(8,128)(2,1)} %all-gather.6.cloned.1.call-done) | copy-start | bytes 39321604
  777.7 19.4 %slice-start = ((s8[13107200]{0:T(1024)(128)(4,1)}), s8[4194304]{0:T(1024)(128)(4,1)S(1)}, s32[]{:S(2)}) async-start(s8[13107200]{0:T(1024)(128)(4,1)} %bitcast.74), calls=%async_computation.3 | async-start | bytes 8388608
  777.7 20.5 %slice-start.1 = ((s8[13107200]{0:T(1024)(128)(4,1)}), s8[4194304]{0:T(1024)(128)(4,1)S(1)}, s32[]{:S(2)}) async-start(s8[13107200]{0:T(1024)(128)(4,1)} %bitcast.74), calls=%async_computation.4 | async-start | bytes 8388608
  790.4 9.1 %slice-start.2 = ((s8[13107200]{0:T(1024)(128)(4,1)}), s8[4194304]{0:T(1024)(128)(4,1)S(1)}, s32[]{:S(2)}) async-start(s8[13107200]{0:T(1024)(128)(4,1)} %bitcast.74), calls=%async_computation.5 | async-start | bytes 8388608
  790.4 9.1 %slice-start.3 = ((s8[13107200]{0:T(1024)(128)(4,1)}), s8[524288]{0:T(1024)(128)(4,1)S(1)}, s32[]{:S(2)}) async-start(s8[13107200]{0:T(1024)(128)(4,1)} %bitcast.74), calls=%async_computation.6 | async-start | bytes 1048576
Sparse Core Ops, SparseCore 0:
  506.9 92.3 all-gather.7
  601.7 86.6 all-gather.5
  691.0 86.6 all-gather.3

commit v2 on v1

--- a/solution.py
+++ b/solution.py
@@ -43,20 +43,12 @@
     return (da * scale + wide * (by_mean * (2.0 / h.shape[-1]))).astype(BF16)
 
 
+def sigmoid(g):
+    return 0.5 * jnp.tanh(0.5 * g) + 0.5
+
+
 def columns(total, step):
     return [(at, min(step, total - at)) for at in range(0, total, step)]
-
-
-def over_columns(total, step, body):
-    whole = total // step
-
-    def one(j, _):
-        body(pl.multiple_of(j * step, step), step)
-        return 0
-
-    lax.fori_loop(0, whole, one, 0)
-    if total % step:
-        body(whole * step, total % step)
 
 
 class Work:
@@ -73,14 +65,12 @@
     ff = wg.shape[2]
 
     def body(a, wg, wu, gate, up, act):
-        def piece(at, size):
+        for at, size in columns(ff, 512):
             cols = pl.ds(at, size)
             g, u = nn(a[...], wg[:, cols]), nn(a[...], wu[:, cols])
             gate[:, cols] = g
             up[:, cols] = u
-            act[:, cols] = (g * jax.nn.sigmoid(g) * u).astype(BF16)
-
-        over_columns(ff, 512, piece)
+            act[:, cols] = (g * sigmoid(g) * u).astype(BF16)
 
     row = lambda width: pl.BlockSpec((rows, width), lambda i: (i, 0))
     weight = once((None, d, ff), lambda i: (n, 0, 0))
@@ -113,7 +103,7 @@
 
 
 def silu_back(g, u, dact):
-    s = jax.nn.sigmoid(g)
+    s = sigmoid(g)
     silu = g * s
     return (dact * u * (s + silu * (1.0 - s))).astype(BF16), (dact * silu).astype(BF16)
 
@@ -123,17 +113,12 @@
     ff = wg.shape[2]
 
     def body(a, dy, wg, wu, wd, act, dgu):
-        def piece(at, size):
+        for at, size in columns(ff, 512):
             cols = pl.ds(at, size)
             g, u = nn(a[...], wg[:, cols]), nn(a[...], wu[:, cols])
             dact = nt(dy[...], wd[cols, :]).astype(BF16).astype(F32)
-            s = jax.nn.sigmoid(g)
-            silu = g * s
-            act[:, cols] = (silu * u).astype(BF16)
-            dgu[0, :, cols] = (dact * u * (s + silu * (1.0 - s))).astype(BF16)
-            dgu[1, :, cols] = (dact * silu).astype(BF16)
-
-        over_columns(ff, 512, piece)
+            act[:, cols] = (g * sigmoid(g) * u).astype(BF16)
+            dgu[0, :, cols], dgu[1, :, cols] = silu_back(g, u, dact)
 
     row = lambda width: pl.BlockSpec((rows, width), lambda i: (i, 0))
     weight = once((None, d, ff), lambda i: (n, 0, 0))
@@ -151,12 +136,10 @@
     ff = wd.shape[1]
 
     def body(dh, wd, gate, up, dgu):
-        def piece(at, size):
+        for at, size in columns(ff, 512):
             cols = pl.ds(at, size)
             dact = nt(dh[...], wd[cols, :]).astype(BF16).astype(F32)
             dgu[0, :, cols], dgu[1, :, cols] = silu_back(gate[:, cols], up[:, cols], dact)
-
-        over_columns(ff, 512, piece)
 
     row = lambda width: pl.BlockSpec((rows, width), lambda i: (i, 0))
     return Work(
@@ -199,26 +182,26 @@
     return Work(
         (ff // tile,),
         [(act, pl.BlockSpec((t, tile), lambda i: (0, i))), (dh, once((t, d), lambda i: (0, 0)))],
-        [((ff, d), BF16, pl.BlockSpec((tile, d), lambda i: (i, 0)))],
+        [((1, ff, d), BF16, pl.BlockSpec((None, tile, d), lambda i: (0, i, 0)))],
         body,
         2 * t * d * ff,
     )
 
 
-def by_gate_up(a, dgu, tile):
+def by_gate_up(a, dgu, tile, which):
     t, d = a.shape
     ff = dgu.shape[2]
-    tiles = ff // tile
+    tiles, low = ff // tile, min(which)
 
     def body(a, dgu, out):
-        out[...] = tn(a[...], dgu[...]).astype(BF16)
+        out[...] = tn(dgu[...], a[...]).astype(BF16).T
 
     return Work(
-        (2 * tiles,),
-        [(a, once((t, d), lambda i: (0, 0))), (dgu, pl.BlockSpec((None, t, tile), lambda i: (i // tiles, 0, i % tiles)))],
-        [((2, d, ff), BF16, pl.BlockSpec((None, d, tile), lambda i: (i // tiles, 0, i % tiles)))],
+        (len(which) * tiles,),
+        [(a, once((t, d), lambda i: (0, 0))), (dgu, pl.BlockSpec((None, t, tile), lambda i: (low + i // tiles, 0, i % tiles)))],
+        [((len(which), d, ff), BF16, pl.BlockSpec((None, d, tile), lambda i: (i // tiles, 0, i % tiles)))],
         body,
-        4 * t * d * ff,
+        2 * len(which) * t * d * ff,
     )
 
 
@@ -337,8 +320,8 @@
 
 
 class First:
-    def __init__(self, term, split):
-        self.term, self.split = term, split
+    def __init__(self, terms, which, split):
+        self.term, self.which, self.split = terms, which, split
 
     def ins(self):
         return [(self.term, ANY)]
@@ -361,7 +344,7 @@
 
             def source(half, at, colour=colour):
                 rows, cols = self.split.part(colour, half)
-                return term.at[at, :, rows, cols] if colour == 0 else term.at[:, at, rows, cols]
+                return term.at[self.which, at, :, rows, cols] if colour == 0 else term.at[self.which, :, at, rows, cols]
 
             axis = colour
             ring = Ring(axis, source, lambda half, s=source, axis=axis: s(half, position()[axis]), scratch[colour * RING_SCRATCH :][:RING_SCRATCH])
@@ -522,6 +505,111 @@
     )(own)
 
 
+class Spread:
+    def __init__(self, block, out, split, colour, send, recv):
+        self.block, self.out, self.split, self.colour, self.send, self.recv = block, out, split, colour, send, recv
+
+    def region(self, stage, half, place):
+        rows, cols = self.split.part(self.colour, half)
+        x, y = position()
+        if stage == 0:
+            x, y = (place, y) if self.colour == 0 else (x, place)
+            return self.out.at[:, x, y, rows, cols]
+        return self.out.at[:, :, place, rows, cols] if self.colour == 0 else self.out.at[:, place, :, rows, cols]
+
+    def message(self, stage, i, arriving=False):
+        axis = self.colour if stage == 0 else 1 - self.colour
+        here = position()[axis]
+        right, left = lax.rem(here + 1, SIDE), lax.rem(here + SIDE - 1, SIDE)
+        sender = here if not arriving else (left if i % 2 == 0 else right)
+        half = (0, 1, 1, 0, 0, 1)[i]
+        owner = sender if i < 4 else lax.rem(sender + (SIDE - 1 if i == 4 else 1), SIDE)
+        region = self.region(stage, half, owner)
+        src = region
+        if stage == 0 and i < 4:
+            rows, cols = self.split.part(self.colour, half)
+            src = self.block.at[:, rows, cols]
+        return pltpu.make_async_remote_copy(
+            src_ref=src,
+            dst_ref=region,
+            send_sem=self.send.at[stage, i],
+            recv_sem=self.recv.at[stage, i],
+            device_id={"dp": along(axis, right if i % 2 == 0 else left)},
+            device_id_type=MESH,
+        )
+
+    def start(self, stage, first):
+        for i in (0, 1) if first else (2, 3):
+            self.message(stage, i).start()
+
+    def hand_on(self, stage):
+        for i in (0, 1):
+            self.message(stage, i, True).wait_recv()
+            self.message(stage, 4 + i).start()
+
+    def arrived(self, stage):
+        for i in (2, 3, 4, 5):
+            self.message(stage, i, True).wait_recv()
+
+    def sent(self):
+        for stage in (0, 1):
+            for i in range(6):
+                self.message(stage, i).wait_send()
+
+
+def gathered(blocks, splits, number):
+    n = len(blocks)
+
+    def kernel(*refs):
+        ins, outs, held = refs[:n], refs[n : 2 * n], refs[2 * n : 3 * n]
+        send, recv, load, store = refs[3 * n :]
+        spreads = [[Spread(ins[k], outs[k], splits[k], c, send.at[k, c], recv.at[k, c]) for c in (0, 1)] for k in range(n)]
+        x, y = position()
+        loads = [lambda k=k: pltpu.make_async_copy(ins[k], held[k], load.at[k]) for k in range(n)]
+        stores = [lambda k=k: pltpu.make_async_copy(held[k], outs[k].at[:, x, y], store.at[k]) for k in range(n)]
+        for k in range(n):
+            loads[k]().start()
+        barrier = pltpu.get_barrier_semaphore()
+        for device in neighbours():
+            pl.semaphore_signal(barrier, inc=1, device_id={"dp": device}, device_id_type=MESH)
+        pl.semaphore_wait(barrier, 4)
+        for k in range(n):
+            for first in (True, False):
+                for spread in spreads[k]:
+                    spread.start(0, first)
+        for k in range(n):
+            loads[k]().wait()
+            stores[k]().start()
+        for k in range(n):
+            for spread in spreads[k]:
+                spread.hand_on(0)
+        for k in range(n):
+            stores[k]().wait()
+            for spread in spreads[k]:
+                spread.arrived(0)
+            for first in (True, False):
+                for spread in spreads[k]:
+                    spread.start(1, first)
+        for k in range(n):
+            for spread in spreads[k]:
+                spread.hand_on(1)
+        for k in range(n):
+            for spread in spreads[k]:
+                spread.arrived(1)
+                spread.sent()
+
+    return pl.pallas_call(
+        kernel,
+        out_shape=[jax.ShapeDtypeStruct((b.shape[0], SIDE, SIDE, *b.shape[1:]), b.dtype) for b in blocks],
+        in_specs=[ANY] * n,
+        out_specs=[ANY] * n,
+        scratch_shapes=[pltpu.VMEM(b.shape, b.dtype) for b in blocks]
+        + [pltpu.SemaphoreType.DMA((n, 2, 2, 6)), pltpu.SemaphoreType.DMA((n, 2, 2, 6)), pltpu.SemaphoreType.DMA((n,)), pltpu.SemaphoreType.DMA((n,))],
+        compiler_params=pltpu.CompilerParams(collective_id=number, has_side_effects=True, vmem_limit_bytes=VMEM_LIMIT),
+        name="gathered",
+    )(*blocks)
+
+
 def adamw(w, m, v, g):
     m = 0.9 * m + 0.1 * g
     v = 0.95 * v + 0.05 * g * g
@@ -536,24 +624,25 @@
         x, dy = x[0], dy[0]
         d, ff = wg.shape[1:]
         wide, tall = Split(d // members, ff, True), Split(ff // members, d, False)
-        square = lambda t: t.reshape(SIDE, SIDE, t.shape[0] // members, t.shape[1])
+        square = lambda t: t.reshape(t.shape[0], SIDE, SIDE, t.shape[1] // members, t.shape[2])
 
         a0 = normed(x)
         [[gate0, up0, act0]] = run(gate_up(a0, wg, wu, 0, 256), name="gate_up_0")
-        [[h1, a1]] = run(down(act0, wd, x, 0, 512), name="down_0")
+        [[h1, a1]] = run(down(act0, wd, x, 0, 256), name="down_0")
         [[act1, dgu1]] = run(last_layer(a1, dy, wg, wu, wd, 1, 256), name="layer_1")
         [[d1]] = run(by_down(act1, dy, 640), name="by_down_1")
-        [[gu1], d1_half] = run(by_gate_up(a1, dgu1, 640), First(square(d1), tall), name="by_gate_up_1", number=1)
+        [[gu1], d1_half] = run(by_gate_up(a1, dgu1, 640, (0, 1)), First(square(d1), 0, tall), name="by_gate_up_1", number=1)
+        gu1 = square(gu1)
         [[dh1, _], d1_sum, g1_half] = run(
-            input_back(dgu1, wg, wu, h1, dy, 1, 256), First(square(gu1[0]), wide), Second(d1_half, tall), name="input_back_1", number=2
+            input_back(dgu1, wg, wu, h1, dy, 1, 256), First(gu1, 0, wide), Second(d1_half, tall), name="input_back_1", number=2
         )
         [[dgu0], g1_sum, u1_half] = run(
-            hidden_back(dh1, wd, gate0, up0, 0, 256), First(square(gu1[1]), wide), Second(g1_half, wide), name="hidden_back_0", number=3
+            hidden_back(dh1, wd, gate0, up0, 0, 256), First(gu1, 1, wide), Second(g1_half, wide), name="hidden_back_0", number=3
         )
         [[d0], u1_sum] = run(by_down(act0, dh1, 640), None, Second(u1_half, wide), name="by_down_0", number=4)
-        [[gu0], d0_half] = run(by_gate_up(a0, dgu0, 640), First(square(d0), tall), name="by_gate_up_0", number=5)
-        d0_sum, g0_half = run(None, First(square(gu0[0]), wide), Second(d0_half, tall), name="sum_gate_0", number=6)
-        g0_sum, u0_half = run(None, First(square(gu0[1]), wide), Second(g0_half, wide), name="sum_up_0", number=7)
+        [[g0], d0_half] = run(by_gate_up(a0, dgu0, 640, (0,)), First(square(d0), 0, tall), name="by_gate_0", number=5)
+        [[u0], d0_sum, g0_half] = run(by_gate_up(a0, dgu0, 640, (1,)), First(square(g0), 0, wide), Second(d0_half, tall), name="by_up_0", number=6)
+        g0_sum, u0_half = run(None, First(square(u0), 0, wide), Second(g0_half, wide), name="sum_up_0", number=7)
         [u0_sum] = run(None, None, Second(u0_half, wide), name="sum_end", number=8)
 
         g = [
@@ -569,9 +658,10 @@
         for w, m, v, one in zip((wg, wu, wd), moments[:3], moments[3:], g, strict=True):
             rows = w.shape[1] // members
             mine = lax.dynamic_slice_in_dim(w, me * rows, rows, 1).astype(F32)
-            w, m, v = adamw(mine, m, v, one * factor)
-            new.append((lax.all_gather(w, "dp", axis=1, tiled=True), m, v))
-        return tuple(one[which] for which in range(3) for one in new)
+            new.append(adamw(mine, m, v, one * factor))
+        weights = gathered([w for w, _, _ in new], (wide, wide, tall), 10)
+        weights = [one.reshape(w.shape) for one, w in zip(weights, (wg, wu, wd), strict=True)]
+        return (*weights, *(m for _, m, _ in new), *(v for _, _, v in new))
 
     parts, whole, moment, out = P(("rep", "dp"), None, None), P(None, None, None), P(None, "dp", None), P("rep", "dp", None)
     return jax.shard_map(

time: 816 us -> 687 us (0.84)
  the two profiles are of different devices: /device:TPU:97 before, /device:TPU:96 now
where the time goes in v2:
time: 687 us; the launch traced here: 677 us
  Pallas kernels  619 us (90%)
  local copies, waits for them, and re-layouts  31.6 us (5%)
  other arithmetic  21.8 us (3%)
    pallas_call x12, Pallas kernels, run(): pl.pallas_call(kernel, out_shape=[jax.ShapeDtypeStruct(shape, kind) for g...  413 us
    pallas_call x1, Pallas kernels, gathered(): pl.pallas_call(kernel, out_shape=[jax.ShapeDtypeStruct((b.shape[0], SIDE,...  198 us
    unnamed x31, local copies, waits for them, and re-layouts  27 us

profile of v2, /device:TPU:96, one launch (start us, length us, event | category | flops | bytes accessed | tf_op | source)
XLA Modules:
  0.0 676.9 jit_solution(14922626064139532169)
XLA Ops:
  0.6 0.0 copy-start
  0.7 3.2 fusion
  3.9 0.2 copy-done
  4.1 2.7 fusion.1.refs_0_
  6.8 38.5 %gate_up_0.1 = (f32[2048,3200]{1,0:T(8,128)}, f32[2048,3200]{1,0:T(8,128)}, bf16[2048,3200]{1,0:T(8,128)(2,1)}) custom-call(bf16[2048,1024]{1,0:T(8,128)(2,1)} %fusion.1.refs_0_, bf16[2,1024,3200]{2,1,0:T(8,128)(2,1)} %refs_1_.6, bf16[2,1024,3200]{2,1,0:T(8,128)(2,1)} %refs_2_.5), custom_call_target="tpu_custom_call" | custom-call | flops 26843545600 | bytes 16777216 | tf_op jit(solution)/shard_map/gate_up_0/pallas_call | solution.py:453
  45.3 21.3 %down_0.1 = (bf16[2048,1024]{1,0:T(8,128)(2,1)}, bf16[2048,1024]{1,0:T(8,128)(2,1)}) custom-call(bf16[2048,3200]{1,0:T(8,128)(2,1)} %get-tuple-element.61.refs_0_, bf16[2,3200,1024]{2,1,0:T(8,128)(2,1)} %refs_1_.7, bf16[2048,1024]{1,0:T(8,128)(2,1)} %bitcast.72), custom_call_target="tpu_custom_call" | custom-call | flops 13421772800 | bytes 16777216 | tf_op jit(solution)/shard_map/down_0/pallas_call | solution.py:453
  66.6 55.4 %layer_1.1 = (bf16[2048,3200]{1,0:T(8,128)(2,1)}, bf16[2,2048,3200]{2,1,0:T(8,128)(2,1)}) custom-call(bf16[2048,1024]{1,0:T(8,128)(2,1)} %get-tuple-element.62.refs_0_, bf16[2048,1024]{1,0:T(8,128)(2,1)} %bitcast.81, bf16[2,1024,3200]{2,1,0:T(8,128)(2,1)} %refs_1_.6, bf16[2,1024,3200]{2,1,0:T(8,128)(2,1)} %refs_2_.5, bf16[2,3200,1024]{2,1,0:T(8,128)(2,1)} %refs_1_.7), custom_call_target="tpu_custom_call" | custom-call | flops 40265318400 | bytes 16777216 | tf_op jit(solution)/shard_map/layer_1/pallas_call | solution.py:453
  122.1 18.6 %by_down_1.1 = bf16[1,3200,1024]{2,1,0:T(8,128)(2,1)} custom-call(bf16[2048,3200]{1,0:T(8,128)(2,1)} %get-tuple-element.65.refs_0_, bf16[2048,1024]{1,0:T(8,128)(2,1)} %bitcast.82), custom_call_target="tpu_custom_call" | custom-call | flops 13421772800 | bytes 16777216 | tf_op jit(solution)/shard_map/by_down_1/pallas_call | solution.py:453
  140.7 41.2 %by_gate_up_1.1 = (bf16[2,1024,3200]{2,1,0:T(8,128)(2,1)}, bf16[2,4,200,256]{3,2,1,0:T(8,128)(2,1)}, f32[2,200,256]{2,1,0:T(8,128)}, bf16[2,4,200,256]{3,2,1,0:T(8,128)(2,1)}, f32[2,200,256]{2,1,0:T(8,128)}) custom-call(bf16[2048,1024]{1,0:T(8,128)(2,1)} %get-tuple-element.62.refs_0_, bf16[2,2048,3200]{2,1,0:T(8,128)(2,1)} %get-tuple-element.63.refs_1_.refs_0_, ...), custom_call_target="tpu_custom_call" | custom-call | flops 26843545600 | bytes 16777216 | tf_op jit(solution)/shard_map/by_gate_up_1/pallas_call | solution.py:453
  181.9 47.3 %input_back_1.1 = (bf16[2048,1024]{1,0:T(8,128)(2,1)}, bf16[2048,1024]{1,0:T(8,128)(2,1)}, bf16[2,200,256]{2,1,0:T(8,128)(2,1)}, bf16[2,200,256]{2,1,0:T(8,128)(...) custom-call(bf16[2,2048,3200]{2,1,0:T(8,128)(2,1)} %get-tuple-elemen, ...), custom_call_target="tpu_custom_call" | custom-call | flops 26843545600 | bytes 16777216 | tf_op jit(solution)/shard_map/input_back_1/pallas_call | solution.py:453
  229.3 46.6 %hidden_back_0.1 = (bf16[2,2048,3200]{2,1,0:T(8,128)(2,1)}, bf16[2,32,1664]{2,1,0:T(8,128)(2,1)}, bf16[2,32,1536]{2,1,0:T(8,128)(2,1)}, bf16[2,4,32,1664]{3,2,1,...) custom-call(bf16[2048,1024]{1,0:T(8,128)(2,1)} %get-tuple-element.71.refs_0_.refs_, ...), custom_call_target="tpu_custom_call" | custom-call | flops 13421772800 | bytes 16777216 | tf_op jit(solution)/shard_map/hidden_back_0/pallas_call | solution.py:453
  275.8 22.2 %by_down_0.1 = (bf16[1,3200,1024]{2,1,0:T(8,128)(2,1)}, bf16[2,32,1664]{2,1,0:T(8,128)(2,1)}, bf16[2,32,1536]{2,1,0:T(8,128)(2,1)}) custom-call(bf16[2048,3200]{1,0:T(8,128)(2,1)} %get-tuple-element.61.refs_0_, bf16[2048,1024]{1,0:T(8,128)(2,1)} %get-tuple-element.71.refs_0_.refs_1_, bf16[2,4,32,1664]{3,2,1,0:T(8,128)(2,1)} %get-tuple-element.79.refs_2_, ...), custom_call_target="tpu_custom_call" | custom-call | flops 13421772800 | bytes 16777216 | tf_op jit(solution)/shard_map/by_down_0/pallas_call | solution.py:453
  298.0 33.8 %by_gate_0.1 = (bf16[1,1024,3200]{2,1,0:T(8,128)(2,1)}, bf16[2,4,200,256]{3,2,1,0:T(8,128)(2,1)}, f32[2,200,256]{2,1,0:T(8,128)}, bf16[2,4,200,256]{3,2,1,0:T(8,128)(2,1)}, f32[2,200,256]{2,1,0:T(8,128)}) custom-call(bf16[2048,1024]{1,0:T(8,128)(2,1)} %fusion.1.refs_0_, bf16[2,2048,3200]{2,1,0:T(8,128)(2,1)} %get-tuple-element.78.refs_1_, ...), custom_call_target="tpu_custom_call" | custom-call | flops 13421772800 | bytes 16777216 | tf_op jit(solution)/shard_map/by_gate_0/pallas_call | solution.py:453
  331.8 41.3 %by_up_0.1 = (bf16[1,1024,3200]{2,1,0:T(8,128)(2,1)}, bf16[2,200,256]{2,1,0:T(8,128)(2,1)}, bf16[2,200,256]{2,1,0:T(8,128)(2,1)}, bf16[2,4,32,1664]{3,2,1,0:T(8,...) custom-call(bf16[2048,1024]{1,0:T(8,128)(2,1)} %fusion.1.refs_0_, ...), custom_call_target="tpu_custom_call" | custom-call | flops 13421772800 | bytes 16777216 | tf_op jit(solution)/shard_map/by_up_0/pallas_call | solution.py:453
  373.1 0.0 copy-start.6
  373.1 0.0 copy-start.5
  373.1 1.0 slice_bitcast_fusion.15
  374.1 1.0 slice_bitcast_fusion.13
  375.2 0.0 copy-done.6
  375.2 0.0 copy-done.5
  375.3 1.0 fusion.13
  376.3 36.0 %sum_up_0.1 = (bf16[2,32,1664]{2,1,0:T(8,128)(2,1)}, bf16[2,32,1536]{2,1,0:T(8,128)(2,1)}, bf16[2,4,32,1664]{3,2,1,0:T(8,128)(2,1)}, f32[2,32,1664]{2,1,0:T(8,12...) custom-call(bf16[2,4,32,1664]{3,2,1,0:T(8,128)(2,1)} %get-tuple-element.89.refs_0_, ...), custom_call_target="tpu_custom_call" | custom-call | flops 1000 | bytes 16777216 | tf_op jit(solution)/shard_map/sum_up_0/pallas_call | solution.py:453
  412.3 0.0 copy-start.3
  412.3 10.5 %sum_end.1 = (bf16[2,32,1664]{2,1,0:T(8,128)(2,1)}, bf16[2,32,1536]{2,1,0:T(8,128)(2,1)}) custom-call(bf16[2,4,32,1664]{3,2,1,0:T(8,128)(2,1)} %get-tuple-element.98.refs_0_, f32[2,32,1664]{2,1,0:T(8,128)} %get-tuple-element.99.refs_1_, bf16[2,4,32,1536]{3,2,1,0:T(8,128)(2,1)} %get-tuple-element.100.refs_2_, f32[2,32,1536]{2,1,0:T(8,128)} %get-tuple-element.101.refs_3_), custom_call_target="tpu_custom_call" | custom-call | flops 1000 | bytes 16777216 | tf_op jit(solution)/shard_map/sum_end/pallas_call | solution.py:453
  422.8 0.0 copy-start.8
  422.8 1.0 slice_bitcast_fusion.3
  423.8 1.0 slice_bitcast_fusion.19
  424.8 0.0 copy-start.4
  424.8 0.0 copy-start.9
  424.8 0.0 copy-done.3
  424.9 0.0 copy-done.8
  424.9 0.0 copy-start.2
  424.9 0.0 copy-start.7
  424.9 1.0 fusion.12
  426.0 0.0 copy-done.4
  426.0 0.0 copy-done.9
  426.1 0.0 copy-done.2
  426.1 0.0 copy-done.7
  426.2 1.0 fusion.11
  429.1 0.6 broadcast_in_dim.4.own
  429.7 8.6 %everywhere.1 = f32[16,8,128]{2,1,0:T(8,128)} custom-call(f32[8,128]{1,0:T(8,128)} %broadcast_in_dim.4.own), custom_call_target="tpu_custom_call" | custom-call | tf_op jit(solution)/shard_map/everywhere/pallas_call | solution.py:497
  438.4 1.5 slice_reduce_fusion
  440.5 4.8 fusion.19
  445.3 6.3 fusion.10
  451.6 198.1 %gathered.1 = (bf16[2,4,4,64,3200]{4,3,2,1,0:T(8,128)(2,1)}, bf16[2,4,4,64,3200]{4,3,2,1,0:T(8,128)(2,1)}, bf16[2,4,4,200,1024]{4,3,2,1,0:T(8,128)(2,1)}) custom-call(bf16[2,64,3200]{2,1,0:T(8,128)(2,1)} %get-tuple-element.119.refs_0_, bf16[2,64,3200]{2,1,0:T(8,128)(2,1)} %get-tuple-element.146.refs_1_, bf16[2,200,1024]{2,1,0:T(8,128)(2,1)} %get-tuple-element.113.refs_2_), custom_call_target="tpu_custom_call" | custom-call | tf_op jit(solution)/shard_map/gathered/pallas_call | solution.py:601
  649.7 0.0 copy-start.1
  649.7 0.0 slice-start
  649.7 0.0 slice-start.1
  649.7 12.7 %copy.23 = bf16[2,1024,3200]{2,1,0:T(8,128)(2,1)} copy(bf16[2,1024,3200]{2,1,0:T(8,128)(2,1)} %bitcast.77) | data formatting | bytes 26214400
  662.4 0.0 copy-done.1
  662.4 0.0 slice-start.2
  662.4 0.0 slice-start.3
  662.4 6.6 copy.24
  669.1 0.0 slice-done
  669.1 1.2 slice-done.1
  670.2 1.3 slice-done.2
  671.5 0.0 slice-done.3
  671.5 4.9 copy.25
  (16 shorter events, 0.4 us)
Async XLA Ops:
  0.6 3.5 copy-start
  373.1 2.0 copy-start.6
  373.1 2.1 copy-start.5
  412.3 12.5 %copy-start.3 = (bf16[2,32,1664]{2,1,0:T(8,128)(2,1)S(1)}, bf16[2,32,1664]{2,1,0:T(8,128)(2,1)}, u32[]{:S(2)}) copy-start(bf16[2,32,1664]{2,1,0:T(8,128)(2,1)} %get-tuple-element.104) | copy-start | bytes 638980
  422.8 2.1 copy-start.8
  424.8 1.2 copy-start.4
  424.8 1.2 copy-start.9
  424.9 1.2 copy-start.2
  424.9 1.2 copy-start.7
  649.7 12.7 %copy-start.1 = (bf16[2,4,4,64,3200]{4,3,2,1,0:T(8,128)(2,1)S(1)}, bf16[2,4,4,64,3200]{4,3,2,1,0:T(8,128)(2,1)}, u32[]{:S(2)}) copy-start(bf16[2,4,4,64,3200]{4,3,2,1,0:T(8,128)(2,1)} %get-tuple-element.111) | copy-start | bytes 39321604
  649.7 19.4 %slice-start = ((s8[13107200]{0:T(1024)(128)(4,1)}), s8[4194304]{0:T(1024)(128)(4,1)S(1)}, s32[]{:S(2)}) async-start(s8[13107200]{0:T(1024)(128)(4,1)} %bitcast.73), calls=%async_computation | async-start | bytes 8388608
  649.7 20.5 %slice-start.1 = ((s8[13107200]{0:T(1024)(128)(4,1)}), s8[4194304]{0:T(1024)(128)(4,1)S(1)}, s32[]{:S(2)}) async-start(s8[13107200]{0:T(1024)(128)(4,1)} %bitcast.73), calls=%async_computation.1 | async-start | bytes 8388608
  662.4 9.1 %slice-start.2 = ((s8[13107200]{0:T(1024)(128)(4,1)}), s8[4194304]{0:T(1024)(128)(4,1)S(1)}, s32[]{:S(2)}) async-start(s8[13107200]{0:T(1024)(128)(4,1)} %bitcast.73), calls=%async_computation.2 | async-start | bytes 8388608
  662.4 9.1 %slice-start.3 = ((s8[13107200]{0:T(1024)(128)(4,1)}), s8[524288]{0:T(1024)(128)(4,1)S(1)}, s32[]{:S(2)}) async-start(s8[13107200]{0:T(1024)(128)(4,1)} %bitcast.73), calls=%async_computation.3 | async-start | bytes 1048576

commit v3 on v2

--- a/solution.py
+++ b/solution.py
@@ -9,6 +9,7 @@
 
 MESH = pl.DeviceIdType.MESH
 ANY = pl.BlockSpec(memory_space=pl.ANY)
+TILE = pl.BlockSpec((8, 128), lambda i: (0, 0))
 VMEM_LIMIT = 62 * 1024 * 1024
 F32, BF16 = jnp.float32, jnp.bfloat16
 SIDE = 4
@@ -51,6 +52,18 @@
     return [(at, min(step, total - at)) for at in range(0, total, step)]
 
 
+def over_columns(total, step, body):
+    whole = total // step
+
+    def one(j, _):
+        body(pl.multiple_of(j * step, step), step)
+        return 0
+
+    lax.fori_loop(0, whole, one, 0)
+    if total % step:
+        body(whole * step, total % step)
+
+
 class Work:
     def __init__(self, grid, ins, outs, body, flops):
         self.grid, self.ins, self.outs, self.body, self.flops = grid, ins, outs, body, flops
@@ -60,11 +73,12 @@
     return pl.BlockSpec(shape, index, pipeline_mode=pl.Buffered(1))
 
 
-def gate_up(a, wg, wu, n, rows):
-    t, d = a.shape
+def gate_up(x, wg, wu, n, rows):
+    t, d = x.shape
     ff = wg.shape[2]
 
-    def body(a, wg, wu, gate, up, act):
+    def body(x, wg, wu, gate, up, act, a):
+        a[...] = normed(x[...])
         for at, size in columns(ff, 512):
             cols = pl.ds(at, size)
             g, u = nn(a[...], wg[:, cols]), nn(a[...], wu[:, cols])
@@ -76,8 +90,8 @@
     weight = once((None, d, ff), lambda i: (n, 0, 0))
     return Work(
         (t // rows,),
-        [(a, row(d)), (wg, weight), (wu, weight)],
-        [((t, ff), F32, row(ff)), ((t, ff), F32, row(ff)), ((t, ff), BF16, row(ff))],
+        [(x, row(d)), (wg, weight), (wu, weight)],
+        [((t, ff), F32, row(ff)), ((t, ff), F32, row(ff)), ((t, ff), BF16, row(ff)), ((t, d), BF16, row(d))],
         body,
         4 * t * d * ff,
     )
@@ -136,10 +150,12 @@
     ff = wd.shape[1]
 
     def body(dh, wd, gate, up, dgu):
-        for at, size in columns(ff, 512):
+        def piece(at, size):
             cols = pl.ds(at, size)
             dact = nt(dh[...], wd[cols, :]).astype(BF16).astype(F32)
             dgu[0, :, cols], dgu[1, :, cols] = silu_back(gate[:, cols], up[:, cols], dact)
+
+        over_columns(ff, 1024, piece)
 
     row = lambda width: pl.BlockSpec((rows, width), lambda i: (i, 0))
     return Work(
@@ -156,9 +172,11 @@
     d = wg.shape[1]
 
     def body(dgu, wg, wu, h, dy, out, da):
-        for at, size in columns(d, 512):
-            cols = slice(at, at + size)
+        def piece(at, size):
+            cols = pl.ds(at, size)
             da[:, cols] = nt(dgu[0], wg[cols, :]).astype(BF16) + nt(dgu[1], wu[cols, :]).astype(BF16)
+
+        over_columns(d, 512, piece)
         out[...] = dy[...] + norm_back(h[...], da[...])
 
     row = lambda width: pl.BlockSpec((rows, width), lambda i: (i, 0))
@@ -241,6 +259,17 @@
     for axis, here in ((0, x), (1, y)):
         for step in (1, SIDE - 1):
             yield along(axis, lax.rem(here + step, SIDE))
+
+
+def over_blocks(out, f, *ins):
+    def one(at, _):
+        out[at] = f(*(i[at] for i in ins)).astype(out.dtype)
+        return 0
+
+    if len(out.shape) == 3:
+        lax.fori_loop(0, out.shape[0], one, 0)
+    else:
+        one(Ellipsis, 0)
 
 
 class Ring:
@@ -291,7 +320,7 @@
         for half in (0, 1):
             self.local(half).wait()
             self.message(half).wait()
-            self.far[half] = (self.far[half].astype(F32) + self.terms[half].astype(F32)).astype(BF16)
+            over_blocks(self.far.at[half], lambda far, term: far.astype(F32) + term.astype(F32), self.far.at[half], self.terms.at[half])
             self.message(4 + half).start()
 
     def finish(self, take):
@@ -352,22 +381,28 @@
         return made
 
     def take(self, ring, out, own, other, half):
-        total = lambda at: ring.mine[half, at].astype(F32) + ring.sums[half, at].astype(F32) + ring.near[half, at].astype(F32)
-        for at in range(SIDE):
-            out[half, at] = total(at).astype(BF16)
-        own[half] = total(position()[other])
+        def total(*terms):
+            return terms[0].astype(F32) + terms[1].astype(F32) + terms[2].astype(F32)
+
+        refs = [r.at[half] for r in (ring.mine, ring.sums, ring.near)]
+        over_blocks(out.at[half], total, *refs)
+        own[half] = total(*(r[position()[other]] for r in refs))
+
+    def after(self, ins, outs):
+        pass
 
 
 class Second:
-    def __init__(self, parts, split):
+    def __init__(self, parts, split, squares):
+        self.squares = squares
         self.parts, self.split = parts, split
 
     def ins(self):
-        return [(p, ANY) for p in self.parts]
+        return [(p, ANY) for p in self.parts] + [(self.squares, TILE)]
 
     def outs(self):
         shapes = [(2, *self.split.piece(colour)) for colour in (0, 1)]
-        return [(shape, BF16, pl.BlockSpec(shape, lambda i: (0, 0, 0))) for shape in shapes]
+        return [(shape, BF16, pl.BlockSpec(shape, lambda i: (0, 0, 0))) for shape in shapes] + [((8, 128), F32, TILE)]
 
     def scratch(self):
         return [s for colour in (0, 1) for s in ring_scratch(self.split.piece(colour), F32)]
@@ -388,8 +423,61 @@
     def take(self, ring, out, half):
         out[half] = (ring.mine[half] + ring.sums[half].astype(F32) + ring.near[half].astype(F32)).astype(BF16)
 
-
-def run(work=None, first=None, second=None, name=None, number=None, relay=(0.3, 0.5)):
+    def after(self, ins, outs):
+        total = ins[4][...]
+        for out in outs[:2]:
+            for half in (0, 1):
+                wide = out[half].astype(F32)
+                total += jnp.sum(jnp.sum(wide * wide, 0, keepdims=True), 1, keepdims=True)
+        outs[2][...] = total
+
+
+class Clip:
+    def __init__(self, members, count):
+        self.members, self.count = members, count
+
+    def ins(self):
+        return []
+
+    def outs(self):
+        return [((8, 128), F32, TILE)]
+
+    def scratch(self):
+        sends = pltpu.SemaphoreType.DMA((self.members - 1,))
+        return [pltpu.VMEM((8, 128), F32), pltpu.VMEM((self.members, 8, 128), F32), sends, sends]
+
+    def peers(self):
+        me = lax.axis_index("dp")
+        return [lax.rem(me + i, self.members) for i in range(1, self.members)]
+
+    def body(self, squares, factor, scratch):
+        own, all_of_them, send, recv = scratch
+        me = lax.axis_index("dp")
+        own[...] = squares
+        all_of_them[me] = squares
+
+        def copy(i, slot):
+            return pltpu.make_async_remote_copy(
+                src_ref=own,
+                dst_ref=all_of_them.at[slot],
+                send_sem=send.at[i],
+                recv_sem=recv.at[i],
+                device_id={"dp": self.peers()[i]},
+                device_id_type=MESH,
+            )
+
+        for i in range(self.members - 1):
+            copy(i, me).start()
+        for i in range(self.members - 1):
+            copy(i, me).wait_send()
+            copy(i, lax.rem(me + self.members - 1 - i, self.members)).wait_recv()
+        total = all_of_them[0]
+        for member in range(1, self.members):
+            total += all_of_them[member]
+        factor[...] = jnp.minimum(1.0, 0.5 * lax.rsqrt(total / self.count + 1e-30))
+
+
+def run(work=None, first=None, second=None, name=None, number=None, relay=(0.3, 0.5), clip=None):
     parts = [p for p in (second, first) if p is not None]
     grid = work.grid if work else (1,)
     steps = grid[0]
@@ -399,6 +487,9 @@
     outs = [list(work.outs)] if work else []
     outs += [p.outs() for p in parts]
     scratch = [p.scratch() for p in parts]
+    if clip:
+        outs.append(clip.outs())
+        scratch.append(clip.scratch())
 
     def cut(refs, sizes):
         made = []
@@ -421,9 +512,10 @@
             @pl.when(step == 0)
             def _():
                 barrier = pltpu.get_barrier_semaphore()
-                for device in neighbours():
+                greeted = clip.peers() if clip else list(neighbours())
+                for device in greeted:
                     pl.semaphore_signal(barrier, inc=1, device_id={"dp": device}, device_id_type=MESH)
-                pl.semaphore_wait(barrier, 4)
+                pl.semaphore_wait(barrier, len(greeted))
                 for first_ones in (True, False):
                     for group in rings:
                         for ring, _ in group:
@@ -449,6 +541,10 @@
                 for group in rings:
                     for ring, take in group:
                         ring.finish(take)
+                for i, part in enumerate(parts):
+                    part.after(in_refs[skip + i], out_refs[skip + i])
+                if clip:
+                    clip.body(out_refs[skip][2][...], out_refs[-1][0], scratch_refs[-1])
 
     made = pl.pallas_call(
         kernel,
@@ -469,40 +565,6 @@
         name=name,
     )(*[a for group in ins for a, _ in group])
     return cut(made, [len(o) for o in outs])
-
-
-def everywhere(own, number, members):
-    def kernel(own, out, send, recv, load):
-        me = lax.axis_index("dp")
-        barrier = pltpu.get_barrier_semaphore()
-        peers = [lax.rem(me + i, members) for i in range(1, members)]
-        for peer in peers:
-            pl.semaphore_signal(barrier, inc=1, device_id={"dp": peer}, device_id_type=MESH)
-        pl.semaphore_wait(barrier, members - 1)
-        keep = pltpu.make_async_copy(own, out.at[me], load)
-        keep.start()
-
-        def copy(i, slot):
-            return pltpu.make_async_remote_copy(
-                src_ref=own, dst_ref=out.at[slot], send_sem=send.at[i], recv_sem=recv.at[i], device_id={"dp": peers[i]}, device_id_type=MESH
-            )
-
-        for i in range(members - 1):
-            copy(i, me).start()
-        keep.wait()
-        for i in range(members - 1):
-            copy(i, me).wait_send()
-            copy(i, lax.rem(me + members - 1 - i, members)).wait_recv()
-
-    return pl.pallas_call(
-        kernel,
-        out_shape=jax.ShapeDtypeStruct((members, *own.shape), own.dtype),
-        in_specs=[ANY],
-        out_specs=pl.BlockSpec(memory_space=pl.ANY),
-        scratch_shapes=[pltpu.SemaphoreType.DMA((members - 1,)), pltpu.SemaphoreType.DMA((members - 1,)), pltpu.SemaphoreType.DMA],
-        compiler_params=pltpu.CompilerParams(collective_id=number, has_side_effects=True),
-        name="everywhere",
-    )(own)
 
 
 class Spread:
@@ -626,33 +688,38 @@
         wide, tall = Split(d // members, ff, True), Split(ff // members, d, False)
         square = lambda t: t.reshape(t.shape[0], SIDE, SIDE, t.shape[1] // members, t.shape[2])
 
-        a0 = normed(x)
-        [[gate0, up0, act0]] = run(gate_up(a0, wg, wu, 0, 256), name="gate_up_0")
+        none = jnp.zeros((8, 128), F32)
+        [[gate0, up0, act0, a0]] = run(gate_up(x, wg, wu, 0, 256), name="gate_up_0")
         [[h1, a1]] = run(down(act0, wd, x, 0, 256), name="down_0")
         [[act1, dgu1]] = run(last_layer(a1, dy, wg, wu, wd, 1, 256), name="layer_1")
         [[d1]] = run(by_down(act1, dy, 640), name="by_down_1")
         [[gu1], d1_half] = run(by_gate_up(a1, dgu1, 640, (0, 1)), First(square(d1), 0, tall), name="by_gate_up_1", number=1)
         gu1 = square(gu1)
-        [[dh1, _], d1_sum, g1_half] = run(
-            input_back(dgu1, wg, wu, h1, dy, 1, 256), First(gu1, 0, wide), Second(d1_half, tall), name="input_back_1", number=2
+        [[dh1, _], [*d1_sum, squares], g1_half] = run(
+            input_back(dgu1, wg, wu, h1, dy, 1, 256), First(gu1, 0, wide), Second(d1_half, tall, none), name="input_back_1", number=2
         )
-        [[dgu0], g1_sum, u1_half] = run(
-            hidden_back(dh1, wd, gate0, up0, 0, 256), First(gu1, 1, wide), Second(g1_half, wide), name="hidden_back_0", number=3
+        [[dgu0], [*g1_sum, squares], u1_half] = run(
+            hidden_back(dh1, wd, gate0, up0, 0, 256), First(gu1, 1, wide), Second(g1_half, wide, squares), name="hidden_back_0", number=3
         )
-        [[d0], u1_sum] = run(by_down(act0, dh1, 640), None, Second(u1_half, wide), name="by_down_0", number=4)
-        [[g0], d0_half] = run(by_gate_up(a0, dgu0, 640, (0,)), First(square(d0), 0, tall), name="by_gate_0", number=5)
-        [[u0], d0_sum, g0_half] = run(by_gate_up(a0, dgu0, 640, (1,)), First(square(g0), 0, wide), Second(d0_half, tall), name="by_up_0", number=6)
-        g0_sum, u0_half = run(None, First(square(u0), 0, wide), Second(g0_half, wide), name="sum_up_0", number=7)
-        [u0_sum] = run(None, None, Second(u0_half, wide), name="sum_end", number=8)
+        [[d0], [*u1_sum, squares]] = run(by_down(act0, dh1, 640), None, Second(u1_half, wide, squares), name="by_down_0", number=4)
+        [[g0], d0_half] = run(by_gate_up(a0, dgu0, 640, (0,)), First(square(d0), 0, tall), name="by_gate_0", number=5, relay=(0.6, 0.8))
+        [[u0], [*d0_sum, squares], g0_half] = run(
+            by_gate_up(a0, dgu0, 640, (1,)),
+            First(square(g0), 0, wide),
+            Second(d0_half, tall, squares),
+            name="by_up_0",
+            number=6,
+            relay=(0.6, 0.8),
+        )
+        [[*g0_sum, squares], u0_half] = run(None, First(square(u0), 0, wide), Second(g0_half, wide, squares), name="sum_up_0", number=7)
+        count = sum(w.size for w in (wg, wu, wd))
+        [[*u0_sum, _], [factor]] = run(None, None, Second(u0_half, wide, squares), name="sum_end", number=8, clip=Clip(members, count))
+        factor = factor[0, 0]
 
         g = [
             jnp.stack([split.join(one) for one in sums]).astype(F32)
             for split, sums in ((wide, (g0_sum, g1_sum)), (wide, (u0_sum, u1_sum)), (tall, (d0_sum, d1_sum)))
         ]
-        squares = jnp.broadcast_to(sum(jnp.sum(one * one) for one in g), (8, 128))
-        squares = jnp.sum(everywhere(squares, 9, members)[:, 0, 0])
-        count = sum(w.size for w in (wg, wu, wd))
-        factor = jnp.minimum(1.0, 0.5 * lax.rsqrt(squares / count + 1e-30))
         me = lax.axis_index("dp")
         new = []
         for w, m, v, one in zip((wg, wu, wd), moments[:3], moments[3:], g, strict=True):

time: 687 us -> 681 us (level)
  other arithmetic: 21.8 us -> 13.9 us
    pallas_call x12, Pallas kernels: 413 us -> 426 us  [run(): pl.pallas_call(kernel, out_shape=[jax.ShapeDtypeStruct(shape, kind) for g...]
    pallas_call x1 -> x0, Pallas kernels: 8.61 us -> none  [everywhere(): pl.pallas_call(kernel, out_shape=jax.ShapeDtypeStruct((members, *own.shap...]
    reduce_sum x5 -> x0, other arithmetic: 7.76 us -> none  [the longest x1 3.22 us: normed(): scale = lax.rsqrt(jnp.mean(wide ** 2, -1, keepdims=True) + 1e-06)]
    unnamed x31 -> x37, local copies, waits for them, and re-layouts: 27 us -> 29 us
where the time goes in v3:
time: 681 us; the launch traced here: 672 us
  Pallas kernels  625 us (92%)
  local copies, waits for them, and re-layouts  32.1 us (5%)
  other arithmetic  13.9 us (2%)
    pallas_call x12, Pallas kernels, run(): pl.pallas_call(kernel, out_shape=[jax.ShapeDtypeStruct(shape, kind) for g...  426 us
    pallas_call x1, Pallas kernels, gathered(): pl.pallas_call(kernel, out_shape=[jax.ShapeDtypeStruct((b.shape[0], SIDE,...  199 us
    unnamed x37, local copies, waits for them, and re-layouts  29 us

profile of v3, /device:TPU:96, one launch (start us, length us, event | category | flops | bytes accessed | tf_op | source)
XLA Modules:
  0.0 672.3 jit_solution(17244094504106626526)
XLA Ops:
  0.6 39.6 %gate_up_0.1 = (f32[2048,3200]{1,0:T(8,128)}, f32[2048,3200]{1,0:T(8,128)}, bf16[2048,3200]{1,0:T(8,128)(2,1)}, bf16[2048,1024]{1,0:T(8,128)(2,1)}) custom-call(bf16[2048,1024]{1,0:T(8,128)(2,1)} %bitcast.79, bf16[2,1024,3200]{2,1,0:T(8,128)(2,1)} %refs_1_.6, bf16[2,1024,3200]{2,1,0:T(8,128)(2,1)} %refs_2_.5), custom_call_target="tpu_custom_call" | custom-call | flops 26843545600 | bytes 16777216 | tf_op jit(solution)/shard_map/gate_up_0/pallas_call | solution.py:549
  40.2 21.3 %down_0.1 = (bf16[2048,1024]{1,0:T(8,128)(2,1)}, bf16[2048,1024]{1,0:T(8,128)(2,1)}) custom-call(bf16[2048,3200]{1,0:T(8,128)(2,1)} %get-tuple-element.69.refs_0_, bf16[2,3200,1024]{2,1,0:T(8,128)(2,1)} %refs_1_.7, bf16[2048,1024]{1,0:T(8,128)(2,1)} %bitcast.80), custom_call_target="tpu_custom_call" | custom-call | flops 13421772800 | bytes 16777216 | tf_op jit(solution)/shard_map/down_0/pallas_call | solution.py:549
  61.5 55.5 %layer_1.1 = (bf16[2048,3200]{1,0:T(8,128)(2,1)}, bf16[2,2048,3200]{2,1,0:T(8,128)(2,1)}) custom-call(bf16[2048,1024]{1,0:T(8,128)(2,1)} %get-tuple-element.70.refs_0_, bf16[2048,1024]{1,0:T(8,128)(2,1)} %bitcast.81, bf16[2,1024,3200]{2,1,0:T(8,128)(2,1)} %refs_1_.6, bf16[2,1024,3200]{2,1,0:T(8,128)(2,1)} %refs_2_.5, bf16[2,3200,1024]{2,1,0:T(8,128)(2,1)} %refs_1_.7), custom_call_target="tpu_custom_call" | custom-call | flops 40265318400 | bytes 16777216 | tf_op jit(solution)/shard_map/layer_1/pallas_call | solution.py:549
  117.0 18.6 %by_down_1.1 = bf16[1,3200,1024]{2,1,0:T(8,128)(2,1)} custom-call(bf16[2048,3200]{1,0:T(8,128)(2,1)} %get-tuple-element.73.refs_0_, bf16[2048,1024]{1,0:T(8,128)(2,1)} %bitcast.82), custom_call_target="tpu_custom_call" | custom-call | flops 13421772800 | bytes 16777216 | tf_op jit(solution)/shard_map/by_down_1/pallas_call | solution.py:549
  135.6 41.4 %by_gate_up_1.1 = (bf16[2,1024,3200]{2,1,0:T(8,128)(2,1)}, bf16[2,4,200,256]{3,2,1,0:T(8,128)(2,1)}, f32[2,200,256]{2,1,0:T(8,128)}, bf16[2,4,200,256]{3,2,1,0:T(8,128)(2,1)}, f32[2,200,256]{2,1,0:T(8,128)}) custom-call(bf16[2048,1024]{1,0:T(8,128)(2,1)} %get-tuple-element.70.refs_0_, bf16[2,2048,3200]{2,1,0:T(8,128)(2,1)} %get-tuple-element.71.refs_1_.refs_0_, ...), custom_call_target="tpu_custom_call" | custom-call | flops 26843545600 | bytes 16777216 | tf_op jit(solution)/shard_map/by_gate_up_1/pallas_call | solution.py:549
  176.9 0.6 broadcast_in_dim.3.refs_9_
  177.5 48.9 %input_back_1.1 = (bf16[2048,1024]{1,0:T(8,128)(2,1)}, bf16[2048,1024]{1,0:T(8,128)(2,1)}, bf16[2,200,256]{2,1,0:T(8,128)(2,1)}, bf16[2,200,256]{2,1,0:T(8,128)(...) custom-call(bf16[2,2048,3200]{2,1,0:T(8,128)(2,1)} %get-tuple-elemen, ...), custom_call_target="tpu_custom_call" | custom-call | flops 26843545600 | bytes 16777216 | tf_op jit(solution)/shard_map/input_back_1/pallas_call | solution.py:549
  226.5 47.0 %hidden_back_0.1 = (bf16[2,2048,3200]{2,1,0:T(8,128)(2,1)}, bf16[2,32,1664]{2,1,0:T(8,128)(2,1)}, bf16[2,32,1536]{2,1,0:T(8,128)(2,1)}, f32[8,128]{1,0:T(8,128)}...) custom-call(bf16[2048,1024]{1,0:T(8,128)(2,1)} %get-tuple-element.79, ...), custom_call_target="tpu_custom_call" | custom-call | flops 13421772800 | bytes 16777216 | tf_op jit(solution)/shard_map/hidden_back_0/pallas_call | solution.py:549
  273.5 20.6 %by_down_0.1 = (bf16[1,3200,1024]{2,1,0:T(8,128)(2,1)}, bf16[2,32,1664]{2,1,0:T(8,128)(2,1)}, bf16[2,32,1536]{2,1,0:T(8,128)(2,1)}, f32[8,128]{1,0:T(8,128)}) custom-call(bf16[2048,3200]{1,0:T(8,128)(2,1)} %get-tuple-element.69.refs_0_, bf16[2048,1024]{1,0:T(8,128)(2,1)} %get-tuple-element.79.refs_0_.refs_1_, ...), custom_call_target="tpu_custom_call" | custom-call | flops 13421772800 | bytes 16777216 | tf_op jit(solution)/shard_map/by_down_0/pallas_call | solution.py:549
  294.1 34.6 %by_gate_0.1 = (bf16[1,1024,3200]{2,1,0:T(8,128)(2,1)}, bf16[2,4,200,256]{3,2,1,0:T(8,128)(2,1)}, f32[2,200,256]{2,1,0:T(8,128)}, bf16[2,4,200,256]{3,2,1,0:T(8,128)(2,1)}, f32[2,200,256]{2,1,0:T(8,128)}) custom-call(bf16[2048,1024]{1,0:T(8,128)(2,1)} %get-tuple-element.68.refs_0_, bf16[2,2048,3200]{2,1,0:T(8,128)(2,1)} %get-tuple-element.87.refs_1_, ...), custom_call_target="tpu_custom_call" | custom-call | flops 13421772800 | bytes 16777216 | tf_op jit(solution)/shard_map/by_gate_0/pallas_call | solution.py:549
  328.7 41.8 %by_up_0.1 = (bf16[1,1024,3200]{2,1,0:T(8,128)(2,1)}, bf16[2,200,256]{2,1,0:T(8,128)(2,1)}, bf16[2,200,256]{2,1,0:T(8,128)(2,1)}, f32[8,128]{1,0:T(8,128)}, bf16...) custom-call(bf16[2048,1024]{1,0:T(8,128)(2,1)} %get-tuple-element.68, ...), custom_call_target="tpu_custom_call" | custom-call | flops 13421772800 | bytes 16777216 | tf_op jit(solution)/shard_map/by_up_0/pallas_call | solution.py:549
  370.4 0.0 copy-start.7
  370.4 0.0 copy-start.8
  370.5 1.1 slice_bitcast_fusion.13
  371.6 0.8 maximum_bitcast_fusion.4
  372.4 0.0 copy-done.7
  372.4 0.0 copy-done.8
  372.4 0.8 maximum_bitcast_fusion.5
  373.2 37.6 %sum_up_0.1 = (bf16[2,32,1664]{2,1,0:T(8,128)(2,1)}, bf16[2,32,1536]{2,1,0:T(8,128)(2,1)}, f32[8,128]{1,0:T(8,128)}, bf16[2,4,32,1664]{3,2,1,0:T(8,128)(2,1)}, f...) custom-call(bf16[2,4,32,1664]{3,2,1,0:T(8,128)(2,1)} %get-tuple-element.100.refs_0_, ...), custom_call_target="tpu_custom_call" | custom-call | flops 1000 | bytes 16777216 | tf_op jit(solution)/shard_map/sum_up_0/pallas_call | solution.py:549
  410.8 0.0 copy-start.1
  410.8 19.3 %sum_end.1 = (bf16[2,32,1664]{2,1,0:T(8,128)(2,1)}, bf16[2,32,1536]{2,1,0:T(8,128)(2,1)}, f32[8,128]{1,0:T(8,128)}, f32[8,128]{1,0:T(8,128)}) custom-call(bf16[2,4,32,1664]{3,2,1,0:T(8,128)(2,1)} %get-tuple-element.110.refs_0_, f32[2,32,1664]{2,1,0:T(8,128)} %get-tuple-element.111.refs_1_, bf16[2,4,32,1536]{3,2,1,0:T(8,128)(2,1)} %get-tuple-element.112.refs_2_, ...), custom_call_target="tpu_custom_call" | custom-call | flops 1000 | bytes 16777216 | tf_op jit(solution)/shard_map/sum_end/pallas_call | solution.py:549
  430.2 1.2 slice.83
  431.4 0.0 copy-done.1
  431.4 0.0 copy-start.6
  431.4 0.0 copy-start.12
  431.4 5.2 fusion.8
  436.6 0.0 copy-start.4
  436.6 0.0 copy-start.10
  436.6 0.0 copy-done.6
  436.6 0.0 copy-start.5
  436.7 0.0 copy-done.12
  436.7 0.0 copy-start.11
  436.7 0.8 copy-done.4
  437.5 0.0 copy-start.3
  437.6 0.1 copy-done.10
  437.6 0.0 copy-start.9
  437.7 0.0 copy-done.5
  437.7 0.0 copy-start.2
  437.8 0.1 copy-done.11
  437.9 0.6 copy-done.3
  438.6 0.1 copy-done.9
  438.7 0.5 copy-done.2
  439.2 6.9 %fusion.2 = (bf16[2,64,3200]{2,1,0:T(8,128)(2,1)}, f32[2,64,3200]{2,1,0:T(8,128)}, f32[2,64,3200]{2,1,0:T(8,128)}, bf16[2,64,3200]{2,1,0:T(8,128)(2,1)}, f32[2,64,3200]{2,1,0:T(8,128)}, /*index=5*/f32[2,64,3200]{2,1,0:T(8,128)}) fusion(bf16[2,1024,3200]{2,1,0:T(8,128)(2,1)} %refs_1_.6, s32[]{:T(128)S(6)} %select_n.7, f32[]{:T(128)} %bitcast.17, ...), kind=kLoop, calls=%fused_computation.11 | loop fusion | flops 16384000 | bytes 18022408 | tf_op jit(solution)/shard_map/convert_element_type | solution.py:679
  446.2 198.9 %gathered.1 = (bf16[2,4,4,64,3200]{4,3,2,1,0:T(8,128)(2,1)}, bf16[2,4,4,64,3200]{4,3,2,1,0:T(8,128)(2,1)}, bf16[2,4,4,200,1024]{4,3,2,1,0:T(8,128)(2,1)}) custom-call(bf16[2,64,3200]{2,1,0:T(8,128)(2,1)} %get-tuple-element.133.refs_0_, bf16[2,64,3200]{2,1,0:T(8,128)(2,1)} %get-tuple-element.160.refs_1_, bf16[2,200,1024]{2,1,0:T(8,128)(2,1)} %get-tuple-element.127.refs_2_), custom_call_target="tpu_custom_call" | custom-call | tf_op jit(solution)/shard_map/gathered/pallas_call | solution.py:663
  645.1 0.0 copy-start
  645.1 0.0 slice-start
  645.1 0.0 slice-start.1
  645.1 12.7 %copy.23 = bf16[2,1024,3200]{2,1,0:T(8,128)(2,1)} copy(bf16[2,1024,3200]{2,1,0:T(8,128)(2,1)} %bitcast.75) | data formatting | bytes 26214400
  657.8 0.0 copy-done
  657.8 0.0 slice-start.2
  657.8 0.0 slice-start.3
  657.8 6.6 copy.24
  664.5 0.0 slice-done
  664.5 1.2 slice-done.1
  665.6 1.3 slice-done.2
  666.9 0.0 slice-done.3
  666.9 4.9 copy.25
  (14 shorter events, 0.3 us)
Async XLA Ops:
  370.4 1.9 copy-start.7
  370.4 1.9 copy-start.8
  410.8 20.6 %copy-start.1 = (f32[2,200,1024]{2,1,0:T(8,128)S(1)}, f32[2,200,1024]{2,1,0:T(8,128)}, u32[]{:S(2)}) copy-start(f32[2,200,1024]{2,1,0:T(8,128)} %param.21) | copy-start | bytes 4915204
  431.4 5.2 copy-start.6
  431.4 5.2 copy-start.12
  436.6 0.9 copy-start.4
  436.6 1.0 copy-start.10
  436.6 1.1 copy-start.5
  436.7 1.2 copy-start.11
  437.5 1.0 copy-start.3
  437.6 1.0 copy-start.9
  437.7 1.5 copy-start.2
  645.1 12.7 %copy-start = (bf16[2,4,4,64,3200]{4,3,2,1,0:T(8,128)(2,1)S(1)}, bf16[2,4,4,64,3200]{4,3,2,1,0:T(8,128)(2,1)}, u32[]{:S(2)}) copy-start(bf16[2,4,4,64,3200]{4,3,2,1,0:T(8,128)(2,1)} %get-tuple-element.125) | copy-start | bytes 39321604
  645.1 19.4 %slice-start = ((s8[13107200]{0:T(1024)(128)(4,1)}), s8[4194304]{0:T(1024)(128)(4,1)S(1)}, s32[]{:S(2)}) async-start(s8[13107200]{0:T(1024)(128)(4,1)} %bitcast.71), calls=%async_computation | async-start | bytes 8388608
  645.1 20.5 %slice-start.1 = ((s8[13107200]{0:T(1024)(128)(4,1)}), s8[4194304]{0:T(1024)(128)(4,1)S(1)}, s32[]{:S(2)}) async-start(s8[13107200]{0:T(1024)(128)(4,1)} %bitcast.71), calls=%async_computation.1 | async-start | bytes 8388608
  657.8 9.1 %slice-start.2 = ((s8[13107200]{0:T(1024)(128)(4,1)}), s8[4194304]{0:T(1024)(128)(4,1)S(1)}, s32[]{:S(2)}) async-start(s8[13107200]{0:T(1024)(128)(4,1)} %bitcast.71), calls=%async_computation.2 | async-start | bytes 8388608
  657.8 9.1 %slice-start.3 = ((s8[13107200]{0:T(1024)(128)(4,1)}), s8[524288]{0:T(1024)(128)(4,1)S(1)}, s32[]{:S(2)}) async-start(s8[13107200]{0:T(1024)(128)(4,1)} %bitcast.71), calls=%async_computation.3 | async-start | bytes 1048576
